TPU v7x, 32 devices: a whole 2x2x4 slice. The times are simulated.
32 devices in a mesh: row: 4 (over x, core), col: 8 (over z, y).
Axes of the slice: x: 2, y: 2, z: 4, core: 2. Of those that a mesh axis runs over, the one named last changes fastest.
Arguments:
- swath: int32 [640, 4096], P('row', 'col'), may hold values from 0 to 1
- coherence: int32 [640, 4096], P('row', 'col'), may hold values from 0 to 7
- phase_counts: int32 [640, 4096], P('row', 'col'), may hold values from 0 to 255
Outputs:
- unwrapped: float32 [640, 4096], P('row', 'col')
All inputs are finite; a program needn't handle non-finite values.
Results may differ from a plain program's by a relative error of at most 0.0012.
Values sent between devices are 32-bit elements; how exact they have to be, the bound alone decides.
No kernel may reach another device: no remote copies, remote signals or barrier semaphores. Data moves between devices by JAX's collectives and lax.ppermute only.
A program may use at most 128 MiB of HBM per device.

v0:
```python
import jax
import jax.numpy as jnp
from jax import lax
from jax.sharding import PartitionSpec as P

GRIDS = 4
LEVELS = 256
NCLASS = 8


damping = 0.8
diag_floor = 0.5
error_floor = 0.5
epsilon = 1e-06
screen_width = 4.0
highest = lax.Precision.HIGHEST


def with_halo(x, sides, width):
    for axis, dim in sides:
        devices, length = (lax.axis_size(axis), x.shape[dim])
        up = [(i, (i + 1) % devices) for i in range(devices - 1)]
        down = [(j, i) for i, j in up]
        last = lax.slice_in_dim(x, length - width, length, axis=dim)
        leading = lax.slice_in_dim(x, 0, width, axis=dim)
        before = lax.ppermute(last, axis, up)
        after = lax.ppermute(leading, axis, down)
        x = jnp.concatenate([before, x, after], axis=dim)
    return x


def from_behind(value, axis, steps):
    count = lax.axis_size(axis)
    leading, last = (max(0, -steps), min(count, count - steps))
    return lax.ppermute(value, axis, [(source, source + steps) for source in range(leading, last)])


def cosine_table(count):
    freq = jnp.arange(count, dtype=jnp.float32)[:, None]
    place = jnp.arange(count, dtype=jnp.float32)[None, :]
    table = jnp.cos(jnp.pi * (place + 0.5) * freq / count) * jnp.sqrt(2.0 / count)
    return jnp.where(freq == 0, table * jnp.sqrt(0.5), table)


def eigen_values(freq, count):
    return 2.0 - 2.0 * jnp.cos(jnp.pi * freq / count)


def product(first, second):
    return jnp.dot(first, second, precision=highest)


def contract_first(first, second):
    return lax.dot_general(first, second, (((0,), (0,)), ((), ())), precision=highest)


def contract_last(first, second):
    return lax.dot_general(first, second, (((1,), (1,)), ((), ())), precision=highest)


def neighbours(estimate):
    return with_halo(estimate, (("row", 0), ("col", 1)), 1)


def weight_diagonal(w_down_pad, w_right_pad):
    return w_down_pad[1:] + w_down_pad[:-1] + w_right_pad[:, 1:] + w_right_pad[:, :-1]


def operate(padded, estimate, w_down_pad, w_right_pad, diagonal):
    beside = (
        w_down_pad[1:] * padded[2:, 1:-1]
        + w_down_pad[:-1] * padded[:-2, 1:-1]
        + w_right_pad[:, 1:] * padded[1:-1, 2:]
        + w_right_pad[:, :-1] * padded[1:-1, :-2]
    )
    return diagonal * estimate - beside


def prolongate(field):
    return jnp.repeat(jnp.repeat(field, 2, axis=0), 2, axis=1)


def coarse_weights(w_down_pad, w_right_pad):
    w_down = w_down_pad[1:]
    w_up = w_down_pad[:-1]
    lower = w_down[1::2, 0::2] + w_down[1::2, 1::2]
    upper = w_up[0:1, 0::2] + w_up[0:1, 1::2]
    w_right = w_right_pad[:, 1:]
    w_left = w_right_pad[:, :-1]
    rightward = w_right[0::2, 1::2] + w_right[1::2, 1::2]
    leftward = w_left[0::2, 0:1] + w_left[1::2, 0:1]
    return (jnp.concatenate([upper, lower], 0), jnp.concatenate([leftward, rightward], 1))


def coarse_solve(source, w_down_pad, w_right_pad):
    rows_here, cols_here = source.shape
    row_count = lax.axis_size("row")
    col_count = lax.axis_size("col")
    grid_rows = rows_here * row_count
    grid_cols = cols_here * col_count
    local = jnp.sum(w_down_pad[1:]) + jnp.sum(w_right_pad[:, 1:])
    total = lax.psum(local, ("row", "col"))
    count = (grid_rows - 1) * grid_cols + grid_rows * (grid_cols - 1)
    mean = total / count + epsilon
    screen = (screen_width / grid_cols) ** 2
    table_x = cosine_table(grid_rows)
    table_y = cosine_table(grid_cols)
    row_index = lax.axis_index("row")
    col_index = lax.axis_index("col")
    strip = lax.all_gather(source, "row", axis=0, tiled=True)
    spectrum = product(table_x, strip)
    spectrum = lax.all_to_all(spectrum, "col", split_axis=0, concat_axis=1, tiled=True)
    spectrum = contract_last(spectrum, table_y)
    block = grid_rows // col_count
    freq_x = (col_index * block + jnp.arange(block, dtype=jnp.int32)).astype(jnp.float32)
    lam_x = eigen_values(freq_x, grid_rows)
    lam_y = eigen_values(jnp.arange(grid_cols, dtype=jnp.float32), grid_cols)
    spectrum = spectrum / (mean * (lam_x[:, None] + lam_y[None, :] + screen))
    values = product(spectrum, table_y)
    values = lax.all_to_all(values, "col", split_axis=1, concat_axis=0, tiled=True)
    strip = contract_first(table_x, values)
    return lax.dynamic_slice_in_dim(strip, row_index * rows_here, rows_here, 0)


def cycle(estimate, source, w_down_pad, w_right_pad, depth, padded):
    if depth == GRIDS:
        return coarse_solve(source, w_down_pad, w_right_pad)
    diagonal = weight_diagonal(w_down_pad, w_right_pad)
    divisor = jnp.maximum(diagonal, diag_floor)
    if estimate is None:
        estimate = damping * source / divisor
    else:
        estimate = (
            estimate
            + damping
            * (source - operate(padded, estimate, w_down_pad, w_right_pad, diagonal))
            / divisor
        )
    padded = neighbours(estimate)
    residual = source - operate(padded, estimate, w_down_pad, w_right_pad, diagonal)
    rows, cols = residual.shape
    coarse_source = residual.reshape(rows // 2, 2, cols // 2, 2).sum(axis=(1, 3))
    down_next, right_next = coarse_weights(w_down_pad, w_right_pad)
    correction = cycle(None, coarse_source, down_next, right_next, depth + 1, None)
    estimate = estimate + prolongate(correction)
    padded = neighbours(estimate)
    return (
        estimate
        + damping
        * (source - operate(padded, estimate, w_down_pad, w_right_pad, diagonal))
        / divisor
    )


def faces(w_down, w_right, slope_down, slope_right):
    flux_down = w_down * slope_down
    flux_right = w_right * slope_right
    above = from_behind(jnp.stack([w_down[-1], flux_down[-1]]), "row", 1)
    before = from_behind(jnp.stack([w_right[:, -1], flux_right[:, -1]]), "col", 1)
    w_down_pad = jnp.concatenate([above[0:1], w_down], 0)
    w_right_pad = jnp.concatenate([before[0][:, None], w_right], 1)
    flux_up = jnp.concatenate([above[1:2], flux_down[:-1]], 0)
    flux_left = jnp.concatenate([before[1][:, None], flux_right[:, :-1]], 1)
    source = flux_up - flux_down + flux_left - flux_right
    return (source, w_down_pad, w_right_pad)


def wrap_steps(difference):
    half = LEVELS // 2
    return (jnp.mod(difference + half, LEVELS) - half) * (2.0 * jnp.pi / LEVELS)


def body(swath, coherence, phase_counts):
    quality = swath.astype(jnp.float32) * (coherence.astype(jnp.float32) / (NCLASS - 1)) ** 2
    counts = phase_counts.astype(jnp.float32)
    below = from_behind(jnp.stack([quality[0], counts[0]]), "row", -1)
    after = from_behind(jnp.stack([quality[:, 0], counts[:, 0]]), "col", -1)
    quality_below = jnp.concatenate([quality[1:], below[0:1]], 0)
    counts_below = jnp.concatenate([counts[1:], below[1:2]], 0)
    quality_after = jnp.concatenate([quality[:, 1:], after[0][:, None]], 1)
    counts_after = jnp.concatenate([counts[:, 1:], after[1][:, None]], 1)
    w_down = jnp.minimum(quality, quality_below)
    w_right = jnp.minimum(quality, quality_after)
    slope_down = wrap_steps(counts_below - counts)
    slope_right = wrap_steps(counts_after - counts)
    source, w_down_pad, w_right_pad = faces(w_down, w_right, slope_down, slope_right)
    first = cycle(None, source, w_down_pad, w_right_pad, 0, None)
    padded = neighbours(first)
    error_down = padded[2:, 1:-1] - first - slope_down
    error_right = padded[1:-1, 2:] - first - slope_right
    reweighted_down = w_down / jnp.maximum(jnp.abs(error_down), error_floor)
    reweighted_right = w_right / jnp.maximum(jnp.abs(error_right), error_floor)
    source, w_down_pad, w_right_pad = faces(
        reweighted_down, reweighted_right, slope_down, slope_right
    )
    return cycle(first, source, w_down_pad, w_right_pad, 0, padded)


def solution(mesh):
    return jax.shard_map(
        body,
        mesh=mesh,
        in_specs=(P("row", "col"), P("row", "col"), P("row", "col")),
        out_specs=P("row", "col"),
        check_vma=False,
    )
```

profile of v0, /device:TPU:2, one launch (start us, length us, event | category | flops | bytes accessed | tf_op | source)
XLA Modules:
  0.0 568.2 jit_solution(13961509552574522512)
XLA Ops:
  12.6 4.3 collective-permute-start.3
  43.3 22.3 %reshape.124 = f32[80,2,256,2]{3,2,1,0:T(8,128)} reshape(f32[160,512]{1,0:T(8,128)S(1)} %fusion.56) | data formatting | bytes 655360 | tf_op jit(solution)/shard_map/reshape | solution.py:142
  65.7 8.8 %reduce_sum.108 = f32[80,256]{1,0:T(8,128)S(1)} reduce(f32[80,2,256,2]{3,2,1,0:T(8,128)} %reshape.124, f32[]{:T(128)} %constant.30.clone.1), dimensions={1,3}, to_apply=%region_0.1 | reduce | flops 61440 | bytes 409604 | tf_op jit(solution)/shard_map/reduce_sum | solution.py:142
  74.6 2.9 collective-permute-start.8
  85.4 4.9 collective-permute-start.11
  92.2 4.8 collective-permute-done.10
  97.1 6.8 %reshape.125 = f32[40,2,128,2]{3,2,1,0:T(8,128)} reshape(f32[80,256]{1,0:T(8,128)S(1)} %fusion.131) | data formatting | bytes 163840 | tf_op jit(solution)/shard_map/reshape | solution.py:142
  103.9 3.2 reduce_sum.109
  114.7 4.5 collective-permute-start.15
  121.1 3.9 collective-permute-done.14
  135.8 3.2 collective-permute-start.19
  140.4 4.2 collective-permute-done.18
  145.8 5.2 all-gather
  152.6 3.9 all-to-all-start
  156.6 42.0 %psum.14 = f32[]{:T(128)} all-reduce(f32[]{:T(128)S(6)} %add.515), channel_id=1, replica_groups=mesh['row'=4,'col'=8] {'row','col'}, use_global_device_ids=true, to_apply=%region_6.7 | all-reduce | flops 1 | bytes 8 | tf_op jit(solution)/shard_map/psum | solution.py:102
  205.1 3.8 all-to-all-start.1
  208.9 6.5 %all-to-all-done.1 = f32[8,1,160]{2,1,0:T(1,128)S(1)} async-done(((f32[8,1,160]{2,1,0:T(1,128)}), f32[8,1,160]{2,1,0:T(1,128)S(1)}, u32[]{:S(2)}, u32[]{:S(2)}) %all-to-all-start.1) | async-done | bytes 5152 | tf_op jit(solution)/shard_map/all_to_all | solution.py:120
  228.1 4.2 collective-permute-done.22
  240.2 4.2 collective-permute-start.27
  245.9 4.2 collective-permute-done.26
  258.1 2.8 collective-permute-start.31
  262.6 4.2 collective-permute-done.30
  275.7 4.0 collective-permute-start.35
  282.6 3.4 collective-permute-done.34
  294.7 4.6 collective-permute-start.41
  301.4 4.0 collective-permute-start.40
  333.1 4.3 collective-permute-done.44
  337.8 22.3 %reshape.136 = f32[80,2,256,2]{3,2,1,0:T(8,128)} reshape(f32[160,512]{1,0:T(8,128)S(1)} %fusion.19) | data formatting | bytes 655360 | tf_op jit(solution)/shard_map/reshape | solution.py:142
  360.1 8.8 %reduce_sum.114 = f32[80,256]{1,0:T(8,128)S(1)} reduce(f32[80,2,256,2]{3,2,1,0:T(8,128)} %reshape.136, f32[]{:T(128)} %constant.30.clone.1), dimensions={1,3}, to_apply=%region_7.8 | reduce | flops 61440 | bytes 409604 | tf_op jit(solution)/shard_map/reduce_sum | solution.py:142
  377.7 4.7 collective-permute-start.49
  384.1 4.2 collective-permute-done.48
  388.5 6.8 %reshape.137 = f32[40,2,128,2]{3,2,1,0:T(8,128)} reshape(f32[80,256]{1,0:T(8,128)S(1)} %fusion.110) | data formatting | bytes 163840 | tf_op jit(solution)/shard_map/reshape | solution.py:142
  395.3 3.2 reduce_sum.115
  405.5 2.9 collective-permute-start.53
  409.9 4.2 collective-permute-done.52
  422.8 2.8 collective-permute-start.57
  427.0 4.2 collective-permute-done.56
  431.7 5.2 all-gather.1
  437.9 3.3 all-to-all-start.2
  443.0 41.4 %psum.15 = f32[]{:T(128)} all-reduce(f32[]{:T(128)S(6)} %add.587), channel_id=1, replica_groups=mesh['row'=4,'col'=8] {'row','col'}, use_global_device_ids=true, to_apply=%region_13.14 | all-reduce | flops 1 | bytes 8 | tf_op jit(solution)/shard_map/psum | solution.py:102
  488.4 10.1 %all_to_all.76 = f32[8,1,160]{2,1,0:T(1,128)S(1)} all-to-all(f32[8,1,160]{2,1,0:T(1,128)S(1)} %reshape.164), channel_id=1, replica_groups=mesh['row'=4,'col'=8] {'col'}, dimensions={0} | all-to-all | bytes 10240 | tf_op jit(solution)/shard_map/all_to_all | solution.py:120
  510.5 4.2 collective-permute-done.60
  522.0 4.2 collective-permute-start.65
  527.7 4.2 collective-permute-done.64
  539.2 2.8 collective-permute-start.69
  543.8 4.2 collective-permute-done.68
  556.2 4.0 collective-permute-start.73
  563.1 3.4 collective-permute-done.72
  (427 shorter events, 235.4 us)
Async XLA Ops:
  2.2 7.9 %collective-permute-start = (f32[2,512]{1,0:T(2,128)S(1)}, f32[2,512]{1,0:T(2,128)S(1)}, u32[]{:S(2)}, u32[]{:S(2)}) collective-permute-start(f32[2,512]{1,0:T(2,128)S(1)} %pad_maximum_fusion.179), channel_id=1, source_target_pairs={{8,0},{16,8},{24,16},{9,1},{17,9},{25,17},{10,2},{18,10},{26,18},{... | collective-permute-start | bytes 12296 | tf_op jit(solution)/shard_map/ppermute | solution.py:35
  4.3 5.5 collective-permute-start.2
  12.6 6.3 %collective-permute-start.3 = (f32[2,160]{1,0:T(2,128)S(1)}, f32[2,160]{1,0:T(2,128)S(1)}, u32[]{:S(2)}, u32[]{:S(2)}) collective-permute-start(f32[2,160]{1,0:T(2,128)S(1)} %pad_maximum_fusion.183), channel_id=1, source_target_pairs={{0,1},{1,2},{2,3},{3,4},{4,5},{5,6},{6,7},{8,9},{9,10},{10,11},{11... | collective-permute-start | bytes 3848 | tf_op jit(solution)/shard_map/ppermute | solution.py:35
  16.9 4.9 collective-permute-start.1
  22.2 10.5 %collective-permute-start.4 = (f32[1,512]{1,0:T(1,128)S(1)}, f32[1,512]{1,0:T(1,128)S(1)}, u32[]{:S(2)}, u32[]{:S(2)}) collective-permute-start(f32[1,512]{1,0:T(1,128)S(1)} %get-tuple-element.45), channel_id=1, source_target_pairs={{8,0},{16,8},{24,16},{9,1},{17,9},{25,17},{10,2},{18,10},{26,18},{... | collective-permute-start | bytes 6152 | tf_op jit(solution)/shard_map/ppermute | solution.py:27
  24.1 8.6 %collective-permute-start.5 = (f32[1,512]{1,0:T(1,128)S(1)}, f32[1,512]{1,0:T(1,128)S(1)}, u32[]{:S(2)}, u32[]{:S(2)}) collective-permute-start(f32[1,512]{1,0:T(1,128)S(1)} %get-tuple-element.44), channel_id=1, source_target_pairs={{0,8},{8,16},{16,24},{1,9},{9,17},{17,25},{2,10},{10,18},{18,26},{... | collective-permute-start | bytes 6152 | tf_op jit(solution)/shard_map/ppermute | solution.py:26
  32.8 10.2 %collective-permute-start.7 = (f32[162,1]{1,0:T(8,128)S(1)}, f32[162,1]{1,0:T(8,128)S(1)}, u32[]{:S(2)}, u32[]{:S(2)}) collective-permute-start(f32[162,1]{1,0:T(8,128)S(1)} %get-tuple-element.32), channel_id=1, source_target_pairs={{0,1},{1,2},{2,3},{3,4},{4,5},{5,6},{6,7},{8,9},{9,10},{10,11},{11... | collective-permute-start | bytes 1952 | tf_op jit(solution)/shard_map/ppermute | solution.py:26
  35.3 7.6 %collective-permute-start.6 = (f32[162,1]{1,0:T(8,128)S(1)}, f32[162,1]{1,0:T(8,128)S(1)}, u32[]{:S(2)}, u32[]{:S(2)}) collective-permute-start(f32[162,1]{1,0:T(8,128)S(1)} %get-tuple-element.31), channel_id=1, source_target_pairs={{1,0},{2,1},{3,2},{4,3},{5,4},{6,5},{7,6},{9,8},{10,9},{11,10},{12... | collective-permute-start | bytes 1952 | tf_op jit(solution)/shard_map/ppermute | solution.py:27
  74.6 10.8 %collective-permute-start.8 = (f32[1,256]{1,0:T(1,128)S(1)}, f32[1,256]{1,0:T(1,128)S(1)}, u32[]{:S(2)}, u32[]{:S(2)}) collective-permute-start(f32[1,256]{1,0:T(1,128)S(1)} %get-tuple-element.67), channel_id=1, source_target_pairs={{8,0},{16,8},{24,16},{9,1},{17,9},{25,17},{10,2},{18,10},{26,18},{... | collective-permute-start | bytes 3080 | tf_op jit(solution)/shard_map/ppermute | solution.py:27
  77.4 7.9 %collective-permute-start.9 = (f32[1,256]{1,0:T(1,128)S(1)}, f32[1,256]{1,0:T(1,128)S(1)}, u32[]{:S(2)}, u32[]{:S(2)}) collective-permute-start(f32[1,256]{1,0:T(1,128)S(1)} %get-tuple-element.66), channel_id=1, source_target_pairs={{0,8},{8,16},{16,24},{1,9},{9,17},{17,25},{2,10},{10,18},{18,26},{... | collective-permute-start | bytes 3080 | tf_op jit(solution)/shard_map/ppermute | solution.py:26
  85.4 6.7 %collective-permute-start.11 = (f32[82,1]{1,0:T(8,128)S(1)}, f32[82,1]{1,0:T(8,128)S(1)}, u32[]{:S(2)}, u32[]{:S(2)}) collective-permute-start(f32[82,1]{1,0:T(8,128)S(1)} %get-tuple-element.57), channel_id=1, source_target_pairs={{0,1},{1,2},{2,3},{3,4},{4,5},{5,6},{6,7},{8,9},{9,10},{10,11},{11... | collective-permute-start | bytes 992 | tf_op jit(solution)/shard_map/ppermute | solution.py:26
  90.4 6.6 %collective-permute-start.10 = (f32[82,1]{1,0:T(8,128)S(1)}, f32[82,1]{1,0:T(8,128)S(1)}, u32[]{:S(2)}, u32[]{:S(2)}) collective-permute-start(f32[82,1]{1,0:T(8,128)S(1)} %get-tuple-element.56), channel_id=1, source_target_pairs={{1,0},{2,1},{3,2},{4,3},{5,4},{6,5},{7,6},{9,8},{10,9},{11,10},{12... | collective-permute-start | bytes 992 | tf_op jit(solution)/shard_map/ppermute | solution.py:27
  107.2 6.2 %collective-permute-start.12 = (f32[1,128]{1,0:T(1,128)S(1)}, f32[1,128]{1,0:T(1,128)S(1)}, u32[]{:S(2)}, u32[]{:S(2)}) collective-permute-start(f32[1,128]{1,0:T(1,128)S(1)} %get-tuple-element.89), channel_id=1, source_target_pairs={{8,0},{16,8},{24,16},{9,1},{17,9},{25,17},{10,2},{18,10},{26,18},{... | collective-permute-start | bytes 1544 | tf_op jit(solution)/shard_map/ppermute | solution.py:27
  114.7 6.4 %collective-permute-start.15 = (f32[42,1]{1,0:T(8,128)S(1)}, f32[42,1]{1,0:T(8,128)S(1)}, u32[]{:S(2)}, u32[]{:S(2)}) collective-permute-start(f32[42,1]{1,0:T(8,128)S(1)} %get-tuple-element.79), channel_id=1, source_target_pairs={{0,1},{1,2},{2,3},{3,4},{4,5},{5,6},{6,7},{8,9},{9,10},{10,11},{11... | collective-permute-start | bytes 512 | tf_op jit(solution)/shard_map/ppermute | solution.py:26
  119.2 5.7 %collective-permute-start.14 = (f32[42,1]{1,0:T(8,128)S(1)}, f32[42,1]{1,0:T(8,128)S(1)}, u32[]{:S(2)}, u32[]{:S(2)}) collective-permute-start(f32[42,1]{1,0:T(8,128)S(1)} %get-tuple-element.78), channel_id=1, source_target_pairs={{1,0},{2,1},{3,2},{4,3},{5,4},{6,5},{7,6},{9,8},{10,9},{11,10},{12... | collective-permute-start | bytes 512 | tf_op jit(solution)/shard_map/ppermute | solution.py:27
  128.6 7.1 %collective-permute-start.16 = (f32[1,64]{1,0:T(1,128)S(1)}, f32[1,64]{1,0:T(1,128)S(1)}, u32[]{:S(2)}, u32[]{:S(2)}) collective-permute-start(f32[1,64]{1,0:T(1,128)S(1)} %get-tuple-element.105), channel_id=1, source_target_pairs={{8,0},{16,8},{24,16},{9,1},{17,9},{25,17},{10,2},{18,10},{26,18},{... | collective-permute-start | bytes 776 | tf_op jit(solution)/shard_map/ppermute | solution.py:27
  130.6 5.2 collective-permute-start.17
  139.0 5.6 collective-permute-start.18
  152.6 46.6 %all-to-all-start = ((f32[8,1,160]{2,1,0:T(1,128)}), f32[8,1,160]{2,1,0:T(1,128)S(1)}, u32[]{:S(2)}, u32[]{:S(2)}) async-start(f32[8,1,160]{2,1,0:T(1,128)} %reshape.158), calls=%async_computation | async-start | bytes 16384 | tf_op jit(solution)/shard_map/all_to_all | solution.py:112
  205.1 10.3 %all-to-all-start.1 = ((f32[8,1,160]{2,1,0:T(1,128)}), f32[8,1,160]{2,1,0:T(1,128)S(1)}, u32[]{:S(2)}, u32[]{:S(2)}) async-start(f32[8,1,160]{2,1,0:T(1,128)} %reshape.160), calls=%async_computation.1 | async-start | bytes 16384 | tf_op jit(solution)/shard_map/all_to_all | solution.py:120
  226.7 5.6 collective-permute-start.22
  240.2 5.7 %collective-permute-start.27 = (f32[42,1]{1,0:T(8,128)S(1)}, f32[42,1]{1,0:T(8,128)S(1)}, u32[]{:S(2)}, u32[]{:S(2)}) collective-permute-start(f32[42,1]{1,0:T(8,128)S(1)} %get-tuple-element.77), channel_id=1, source_target_pairs={{0,1},{1,2},{2,3},{3,4},{4,5},{5,6},{6,7},{8,9},{9,10},{10,11},{11... | collective-permute-start | bytes 512 | tf_op jit(solution)/shard_map/ppermute | solution.py:26
  244.4 5.7 %collective-permute-start.26 = (f32[42,1]{1,0:T(8,128)S(1)}, f32[42,1]{1,0:T(8,128)S(1)}, u32[]{:S(2)}, u32[]{:S(2)}) collective-permute-start(f32[42,1]{1,0:T(8,128)S(1)} %get-tuple-element.76), channel_id=1, source_target_pairs={{1,0},{2,1},{3,2},{4,3},{5,4},{6,5},{7,6},{9,8},{10,9},{11,10},{12... | collective-permute-start | bytes 512 | tf_op jit(solution)/shard_map/ppermute | solution.py:27
  260.9 5.9 %collective-permute-start.30 = (f32[82,1]{1,0:T(8,128)S(1)}, f32[82,1]{1,0:T(8,128)S(1)}, u32[]{:S(2)}, u32[]{:S(2)}) collective-permute-start(f32[82,1]{1,0:T(8,128)S(1)} %get-tuple-element.54), channel_id=1, source_target_pairs={{1,0},{2,1},{3,2},{4,3},{5,4},{6,5},{7,6},{9,8},{10,9},{11,10},{12... | collective-permute-start | bytes 992 | tf_op jit(solution)/shard_map/ppermute | solution.py:27
  275.7 6.9 %collective-permute-start.35 = (f32[162,1]{1,0:T(8,128)S(1)}, f32[162,1]{1,0:T(8,128)S(1)}, u32[]{:S(2)}, u32[]{:S(2)}) collective-permute-start(f32[162,1]{1,0:T(8,128)S(1)} %get-tuple-element.30), channel_id=1, source_target_pairs={{0,1},{1,2},{2,3},{3,4},{4,5},{5,6},{6,7},{8,9},{9,10},{10,11},{11... | collective-permute-start | bytes 1952 | tf_op jit(solution)/shard_map/ppermute | solution.py:26
  279.7 6.4 %collective-permute-start.34 = (f32[162,1]{1,0:T(8,128)S(1)}, f32[162,1]{1,0:T(8,128)S(1)}, u32[]{:S(2)}, u32[]{:S(2)}) collective-permute-start(f32[162,1]{1,0:T(8,128)S(1)} %get-tuple-element.29), channel_id=1, source_target_pairs={{1,0},{2,1},{3,2},{4,3},{5,4},{6,5},{7,6},{9,8},{10,9},{11,10},{12... | collective-permute-start | bytes 1952 | tf_op jit(solution)/shard_map/ppermute | solution.py:27
  293.4 6.4 %collective-permute-start.39 = (f32[162,1]{1,0:T(8,128)S(1)}, f32[162,1]{1,0:T(8,128)S(1)}, u32[]{:S(2)}, u32[]{:S(2)}) collective-permute-start(f32[162,1]{1,0:T(8,128)S(1)} %get-tuple-element.27), channel_id=1, source_target_pairs={{1,0},{2,1},{3,2},{4,3},{5,4},{6,5},{7,6},{9,8},{10,9},{11,10},{12... | collective-permute-start | bytes 1952 | tf_op jit(solution)/shard_map/ppermute | solution.py:27
  294.7 26.7 %collective-permute-start.41 = (f32[162,1]{1,0:T(8,128)S(1)}, f32[162,1]{1,0:T(8,128)S(1)}, u32[]{:S(2)}, u32[]{:S(2)}) collective-permute-start(f32[162,1]{1,0:T(8,128)S(1)} %get-tuple-element.28), channel_id=1, source_target_pairs={{0,1},{1,2},{2,3},{3,4},{4,5},{5,6},{6,7},{8,9},{9,10},{10,11},{11... | collective-permute-start | bytes 1952 | tf_op jit(solution)/shard_map/ppermute | solution.py:26
  301.4 17.3 %collective-permute-start.40 = (f32[2,160]{1,0:T(2,128)S(1)}, f32[2,160]{1,0:T(2,128)S(1)}, u32[]{:S(2)}, u32[]{:S(2)}) collective-permute-start(f32[2,160]{1,0:T(2,128)S(1)} %pad_maximum_fusion.184), channel_id=1, source_target_pairs={{0,1},{1,2},{2,3},{3,4},{4,5},{5,6},{6,7},{8,9},{9,10},{10,11},{11... | collective-permute-start | bytes 3848 | tf_op jit(solution)/shard_map/ppermute | solution.py:35
  316.5 4.9 collective-permute-start.37
  324.0 4.9 collective-permute-start.43
  331.0 6.4 %collective-permute-start.44 = (f32[162,1]{1,0:T(8,128)S(1)}, f32[162,1]{1,0:T(8,128)S(1)}, u32[]{:S(2)}, u32[]{:S(2)}) collective-permute-start(f32[162,1]{1,0:T(8,128)S(1)} %get-tuple-element.25), channel_id=1, source_target_pairs={{1,0},{2,1},{3,2},{4,3},{5,4},{6,5},{7,6},{9,8},{10,9},{11,10},{12... | collective-permute-start | bytes 1952 | tf_op jit(solution)/shard_map/ppermute | solution.py:27
  369.0 8.6 %collective-permute-start.46 = (f32[1,256]{1,0:T(1,128)S(1)}, f32[1,256]{1,0:T(1,128)S(1)}, u32[]{:S(2)}, u32[]{:S(2)}) collective-permute-start(f32[1,256]{1,0:T(1,128)S(1)} %get-tuple-element.63), channel_id=1, source_target_pairs={{8,0},{16,8},{24,16},{9,1},{17,9},{25,17},{10,2},{18,10},{26,18},{... | collective-permute-start | bytes 3080 | tf_op jit(solution)/shard_map/ppermute | solution.py:27
  370.9 6.6 %collective-permute-start.47 = (f32[1,256]{1,0:T(1,128)S(1)}, f32[1,256]{1,0:T(1,128)S(1)}, u32[]{:S(2)}, u32[]{:S(2)}) collective-permute-start(f32[1,256]{1,0:T(1,128)S(1)} %get-tuple-element.62), channel_id=1, source_target_pairs={{0,8},{8,16},{16,24},{1,9},{9,17},{17,25},{2,10},{10,18},{18,26},{... | collective-permute-start | bytes 3080 | tf_op jit(solution)/shard_map/ppermute | solution.py:26
  377.7 6.5 %collective-permute-start.49 = (f32[82,1]{1,0:T(8,128)S(1)}, f32[82,1]{1,0:T(8,128)S(1)}, u32[]{:S(2)}, u32[]{:S(2)}) collective-permute-start(f32[82,1]{1,0:T(8,128)S(1)} %get-tuple-element.53), channel_id=1, source_target_pairs={{0,1},{1,2},{2,3},{3,4},{4,5},{5,6},{6,7},{8,9},{9,10},{10,11},{11... | collective-permute-start | bytes 992 | tf_op jit(solution)/shard_map/ppermute | solution.py:26
  382.4 5.9 %collective-permute-start.48 = (f32[82,1]{1,0:T(8,128)S(1)}, f32[82,1]{1,0:T(8,128)S(1)}, u32[]{:S(2)}, u32[]{:S(2)}) collective-permute-start(f32[82,1]{1,0:T(8,128)S(1)} %get-tuple-element.52), channel_id=1, source_target_pairs={{1,0},{2,1},{3,2},{4,3},{5,4},{6,5},{7,6},{9,8},{10,9},{11,10},{12... | collective-permute-start | bytes 992 | tf_op jit(solution)/shard_map/ppermute | solution.py:27
  398.6 5.0 collective-permute-start.50
  408.4 5.7 %collective-permute-start.52 = (f32[42,1]{1,0:T(8,128)S(1)}, f32[42,1]{1,0:T(8,128)S(1)}, u32[]{:S(2)}, u32[]{:S(2)}) collective-permute-start(f32[42,1]{1,0:T(8,128)S(1)} %get-tuple-element.74), channel_id=1, source_target_pairs={{1,0},{2,1},{3,2},{4,3},{5,4},{6,5},{7,6},{9,8},{10,9},{11,10},{12... | collective-permute-start | bytes 512 | tf_op jit(solution)/shard_map/ppermute | solution.py:27
  415.9 5.5 collective-permute-start.54
  425.6 5.6 collective-permute-start.56
  437.9 47.1 %all-to-all-start.2 = ((f32[8,1,160]{2,1,0:T(1,128)}), f32[8,1,160]{2,1,0:T(1,128)S(1)}, u32[]{:S(2)}, u32[]{:S(2)}) async-start(f32[8,1,160]{2,1,0:T(1,128)} %reshape.162), calls=%async_computation.2 | async-start | bytes 16384 | tf_op jit(solution)/shard_map/all_to_all | solution.py:112
  509.1 5.6 collective-permute-start.60
  522.0 5.8 %collective-permute-start.65 = (f32[42,1]{1,0:T(8,128)S(1)}, f32[42,1]{1,0:T(8,128)S(1)}, u32[]{:S(2)}, u32[]{:S(2)}) collective-permute-start(f32[42,1]{1,0:T(8,128)S(1)} %get-tuple-element.73), channel_id=1, source_target_pairs={{0,1},{1,2},{2,3},{3,4},{4,5},{5,6},{6,7},{8,9},{9,10},{10,11},{11... | collective-permute-start | bytes 512 | tf_op jit(solution)/shard_map/ppermute | solution.py:26
  526.2 5.7 %collective-permute-start.64 = (f32[42,1]{1,0:T(8,128)S(1)}, f32[42,1]{1,0:T(8,128)S(1)}, u32[]{:S(2)}, u32[]{:S(2)}) collective-permute-start(f32[42,1]{1,0:T(8,128)S(1)} %get-tuple-element.72), channel_id=1, source_target_pairs={{1,0},{2,1},{3,2},{4,3},{5,4},{6,5},{7,6},{9,8},{10,9},{11,10},{12... | collective-permute-start | bytes 512 | tf_op jit(solution)/shard_map/ppermute | solution.py:27
  542.1 5.9 %collective-permute-start.68 = (f32[82,1]{1,0:T(8,128)S(1)}, f32[82,1]{1,0:T(8,128)S(1)}, u32[]{:S(2)}, u32[]{:S(2)}) collective-permute-start(f32[82,1]{1,0:T(8,128)S(1)} %get-tuple-element.50), channel_id=1, source_target_pairs={{1,0},{2,1},{3,2},{4,3},{5,4},{6,5},{7,6},{9,8},{10,9},{11,10},{12... | collective-permute-start | bytes 992 | tf_op jit(solution)/shard_map/ppermute | solution.py:27
  551.2 4.9 collective-permute-start.71
  556.2 6.9 %collective-permute-start.73 = (f32[162,1]{1,0:T(8,128)S(1)}, f32[162,1]{1,0:T(8,128)S(1)}, u32[]{:S(2)}, u32[]{:S(2)}) collective-permute-start(f32[162,1]{1,0:T(8,128)S(1)} %get-tuple-element.24), channel_id=1, source_target_pairs={{0,1},{1,2},{2,3},{3,4},{4,5},{5,6},{6,7},{8,9},{9,10},{10,11},{11... | collective-permute-start | bytes 1952 | tf_op jit(solution)/shard_map/ppermute | solution.py:26
  560.2 6.4 %collective-permute-start.72 = (f32[162,1]{1,0:T(8,128)S(1)}, f32[162,1]{1,0:T(8,128)S(1)}, u32[]{:S(2)}, u32[]{:S(2)}) collective-permute-start(f32[162,1]{1,0:T(8,128)S(1)} %get-tuple-element.23), channel_id=1, source_target_pairs={{1,0},{2,1},{3,2},{4,3},{5,4},{6,5},{7,6},{9,8},{10,9},{11,10},{12... | collective-permute-start | bytes 1952 | tf_op jit(solution)/shard_map/ppermute | solution.py:27
  (38 other events, 723.4 us)
where the time goes:
time: 577 us; the launch traced here: 568 us
  starting transfers between devices  182 us (32%)
  waiting for transfers between devices  111 us (19%)
  local copies, waits for them, and re-layouts  108 us (19%)
  blocking collectives  104 us (18%)
  other arithmetic  48.4 us (8%)
  matrix products  8.54 us (1%)
  between operations  6.31 us (1%)
    ppermute x34, starting transfers between devices, with_halo(): before = lax.ppermute(last, axis, up)  99.5 us
    psum x2, blocking collectives, coarse_solve(): total = lax.psum(local, ('row', 'col'))  83.4 us
    ppermute x34, waiting for transfers between devices, with_halo(): after = lax.ppermute(leading, axis, down)  62.5 us
    reshape x8, local copies, waits for them, and re-layouts, cycle(): residual.reshape(rows // 2, 2, cols // 2, 2).sum(axis=(1, 3))  62.1 us
    ppermute x34, starting transfers between devices, with_halo(): after = lax.ppermute(leading, axis, down)  56.4 us
    ppermute x34, waiting for transfers between devices, with_halo(): before = lax.ppermute(last, axis, up)  34.1 us
    reduce_sum x8, other arithmetic, cycle(): residual.reshape(rows // 2, 2, cols // 2, 2).sum(axis=(1, 3))  24.7 us
    slice x16, local copies, waits for them, and re-layouts, coarse_weights(): rightward = w_right[0::2, 1::2] + w_right[1::2, 1::2]  16.9 us
  transfers between devices with their start and end apart: 77, of which 45 were waited for; matrix products, arithmetic and copies ran while one was open for 8% of the time, Pallas kernels for 0%

commit v1 on v0

v1 whole, which is shorter than its diff:
```python
import functools

import jax
import jax.numpy as jnp
import numpy as np
from jax import lax
from jax.experimental import pallas as pl
from jax.experimental.pallas import tpu as pltpu
from jax.sharding import PartitionSpec as P

GRIDS = 4
LEVELS = 256
NCLASS = 8

damping = 0.8
diag_floor = 0.5
error_floor = 0.5
epsilon = 1e-06
screen_width = 4.0
highest = lax.Precision.HIGHEST

CELL = 2**GRIDS
ROW_HALO = 3 * CELL
COL_HALO = 64
SUB = 8
LANE = 128


class Shape:
    def __init__(self, rows, cols, row_count, col_count):
        self.rows, self.cols = rows, cols
        self.row_count, self.col_count = row_count, col_count
        unit = SUB * CELL
        self.ext_rows = -(-(rows + 2 * ROW_HALO) // unit) * unit
        self.lanes = cols + 2 * COL_HALO
        self.chunk = self.ext_rows // SUB
        self.tiles = cols // LANE
        self.crows, self.ccols = rows // CELL, cols // CELL
        self.per_chunk = self.chunk // CELL
        self.grid_rows = self.crows * row_count
        self.grid_cols = self.ccols * col_count

    def slabs(self, depth):
        return self.chunk >> depth


def quality_of(swath, coherence):
    scaled = coherence.astype(jnp.float32) / (NCLASS - 1)
    return swath.astype(jnp.float32) * (scaled * scaled)


def lane_index(width):
    return lax.broadcasted_iota(jnp.int32, (SUB, width), 1)


def right_of(x, steps):
    return pltpu.roll(x, x.shape[1] - steps, 1)


def left_of(x, steps):
    return pltpu.roll(x, steps, 1)


def chunk_below(x):
    return pltpu.roll(x, SUB - 1, 0)


def chunk_above(x):
    return pltpu.roll(x, 1, 0)


def wrap_steps(difference):
    turns = jnp.floor(difference * (1.0 / LEVELS) + 0.5)
    return (difference - LEVELS * turns) * (2.0 * jnp.pi / LEVELS)


def relax_weight(diagonal):
    return damping / jnp.maximum(diagonal, diag_floor)


def row_strip_kernel(swath, coherence, counts, top, bottom):
    rows = swath.shape[0]
    for start, out in ((0, top), (rows - ROW_HALO, bottom)):
        here = slice(start, start + ROW_HALO)
        out[0:ROW_HALO, :] = quality_of(swath[here, :], coherence[here, :])
        out[ROW_HALO : 2 * ROW_HALO, :] = counts[here, :].astype(jnp.float32)


def col_strip_kernel(swath, coherence, counts, above, below, first, last, *, shape):
    rows, cols, ext = shape.rows, shape.cols, shape.ext_rows
    low = lax.broadcasted_iota(jnp.int32, (1, LANE), 1) < COL_HALO

    def put(where, quality, phase):
        first[where, :] = jnp.where(low, quality[0], pltpu.roll(phase[0], COL_HALO, 1))
        last[where, :] = jnp.where(low, pltpu.roll(phase[1], COL_HALO, 1), quality[1])

    sides = (slice(0, LANE), slice(cols - LANE, cols))
    put(
        slice(0, rows),
        [quality_of(swath[:, s], coherence[:, s]) for s in sides],
        [counts[:, s].astype(jnp.float32) for s in sides],
    )
    for ref, start in ((below, rows), (above, ext - ROW_HALO)):
        put(
            slice(start, start + ROW_HALO),
            [ref[0:ROW_HALO, s] for s in sides],
            [ref[ROW_HALO : 2 * ROW_HALO, s] for s in sides],
        )
    if ext > rows + 2 * ROW_HALO:
        gap = slice(rows + ROW_HALO, ext - ROW_HALO)
        first[gap, :] = jnp.zeros_like(first[gap, :])
        last[gap, :] = jnp.zeros_like(last[gap, :])


def pair_sum(x, steps, odd):
    y = x + right_of(x, steps)
    return jnp.where(odd, left_of(y, steps), y)


def odd_value(x, steps, odd):
    return jnp.where(odd, x, right_of(x, steps))


def go_down(fine, coarse, depth, shape):
    steps = 1 << depth
    count = shape.slabs(depth + 1)
    odd = (lane_index(shape.lanes) & steps) != 0
    a_f, b_f, gd_f, gr_f, v_f = (fine[k] for k in ("a", "b", "gd", "gr", "est"))
    last_level = depth + 1 == GRIDS
    wrapped = chunk_below(v_f[0])

    def down_part(k, v_next):
        a = a_f[2 * k + 1]
        flux = gd_f[2 * k + 1] + a * (v_next - v_f[2 * k + 1])
        return pair_sum(a, steps, odd), pair_sum(flux, steps, odd)

    def step(k, v_next, a_prev, gd_prev):
        a, gd = down_part(k, v_next)
        v0, v1 = v_f[2 * k], v_f[2 * k + 1]
        b0, b1 = b_f[2 * k], b_f[2 * k + 1]
        fr = gr_f[2 * k] + gr_f[2 * k + 1] + b0 * (right_of(v0, steps) - v0) + b1 * (right_of(v1, steps) - v1)
        b = odd_value(b0 + b1, steps, odd)
        gr = odd_value(fr, steps, odd)
        right_side = gd - gd_prev + gr - left_of(gr, 2 * steps)
        if last_level:
            coarse["w"][k] = a + b
            coarse["est"][k] = right_side
        else:
            w = relax_weight(a + a_prev + b + left_of(b, 2 * steps))
            coarse["a"][k] = a
            coarse["b"][k] = b
            coarse["gd"][k] = gd
            coarse["gr"][k] = gr
            coarse["w"][k] = w
            coarse["est"][k] = w * right_side
        return a, gd

    a, gd = down_part(count - 1, wrapped)
    carry = (chunk_above(a), chunk_above(gd))
    carry = lax.fori_loop(0, count - 1, lambda k, c: step(k, v_f[2 * k + 2], *c), carry)
    step(count - 1, wrapped, *carry)


def lane_select(shape):
    place = lax.broadcasted_iota(jnp.int32, (shape.cols, LANE), 0)
    target = lax.broadcasted_iota(jnp.int32, (shape.cols, LANE), 1)
    return (place == target * CELL).astype(jnp.bfloat16)


def three_parts(x):
    high = x.astype(jnp.bfloat16)
    rest = x - high.astype(jnp.float32)
    middle = rest.astype(jnp.bfloat16)
    low = (rest - middle.astype(jnp.float32)).astype(jnp.bfloat16)
    return high, middle, low


def select_product(x, one_hot):
    n = x.shape[0]
    parts = jnp.concatenate(list(three_parts(x)), axis=0)
    out = jnp.dot(parts, one_hot, preferred_element_type=jnp.float32)
    return out[0:n] + out[n : 2 * n] + out[2 * n : 3 * n]


def publish(coarse, out, shape):
    per = shape.per_chunk
    weights = sum(coarse["w"][j][:, : shape.cols] for j in range(per))
    fields = [coarse["est"][j][:, : shape.cols] for j in range(per)] + [weights]
    packed = select_product(jnp.concatenate(fields, axis=0), lane_select(shape))
    block = packed[0:SUB]
    for j in range(1, per + 1):
        block = block + pltpu.roll(packed[j * SUB : (j + 1) * SUB], j * shape.ccols, 1)
    for device in range(shape.row_count * shape.col_count):
        out[device] = block


LEVEL_KEYS = ("a", "b", "gd", "gr", "w", "est")


def levels_down(level0, levels, last, out, shape):
    chain = [level0] + levels + [last]
    for depth in range(GRIDS):
        go_down(chain[depth], chain[depth + 1], depth, shape)
    publish(last, out, shape)


def coarse_correction(gathered, table, shape, corr):
    rows, cols = shape.row_count, shape.col_count
    per, crows, ccols = shape.per_chunk, shape.crows, shape.ccols
    gr, gc = shape.grid_rows, shape.grid_cols
    group = LANE // ccols
    lane = lane_index(LANE)
    blocks = []
    for j in range(per):
        for r in range(rows):
            pieces = []
            for tile in range(cols // group):
                piece = None
                for g in range(group):
                    x = gathered[r * cols + tile * group + g]
                    shift = ((g - j) * ccols) % LANE
                    x = pltpu.roll(x, shift, 1) if shift else x
                    piece = x if piece is None else jnp.where(lane >= g * ccols, x, piece)
                pieces.append(piece)
            blocks.append(jnp.concatenate(pieces, axis=1))
    strip = jnp.concatenate(blocks, axis=0)

    weights = gathered[0]
    for device in range(1, rows * cols):
        weights = weights + gathered[device]
    sub = lax.broadcasted_iota(jnp.int32, (SUB, LANE), 0)
    own = (sub < crows // per) & (lane >= per * ccols) & (lane < (per + 1) * ccols)
    total = jnp.sum(jnp.where(own, weights, 0.0), keepdims=True)
    count = (gr - 1) * gc + gr * (gc - 1)
    mean = total / count + epsilon

    def at(dim, size):
        return lax.broadcasted_iota(jnp.int32, size, dim)

    def cosines(freq, place):
        value = jnp.cos((jnp.pi / gr) * ((place.astype(jnp.float32) + 0.5) * freq.astype(jnp.float32)))
        return jnp.where(freq == 0, np.float32(np.sqrt(1.0 / gr)), np.float32(np.sqrt(2.0 / gr)) * value)

    size = (gr, per * rows * SUB)
    column = at(1, size)
    chunk = column % SUB
    place = (column // SUB) % rows * crows + chunk * per + column // (SUB * rows)
    inside = chunk < crows // per
    forward_x = jnp.where(inside, cosines(at(0, size), jnp.where(inside, place, 0)), 0.0)

    size = (per * SUB, gr)
    slot = (at(0, size) % SUB) * per + at(0, size) // SUB
    slots = SUB * per
    local = jnp.where(slot < slots - ROW_HALO // CELL, slot, slot - slots)
    backward_x = cosines(at(1, size), lax.axis_index("row") * crows + local)

    spectrum = lax.dot_general(strip, table[...], (((1,), (1,)), ((), ())), precision=highest)
    spectrum = jnp.dot(forward_x, spectrum, precision=highest)
    size = (gr, gc)

    def eigen(index, n):
        return 2.0 - 2.0 * jnp.cos((jnp.pi / n) * index.astype(jnp.float32))

    lam = eigen(at(0, (gr, 1)), gr) + eigen(at(1, (1, gc)), gc)
    screen = (screen_width / gc) ** 2
    spectrum = spectrum / (mean * (lam + screen))
    values = jnp.dot(backward_x, spectrum, precision=highest)
    values = jnp.dot(values, table[...], precision=highest)

    size = (gc, shape.lanes)
    cell = at(1, size) // CELL
    edge = (shape.cols + COL_HALO) // CELL
    cell = jnp.where(cell < edge, cell, cell - shape.lanes // CELL)
    spread = (at(0, size) == cell + lax.axis_index("col") * ccols).astype(jnp.bfloat16)
    values = select_product(values, spread)
    for j in range(per):
        corr[j] = values[j * SUB : (j + 1) * SUB]


def go_up(level, corr, depth, shape, emit):
    steps = 1 << depth
    count = shape.slabs(depth)
    a_r, b_r, gd_r, gr_r, w_r, e_r = (level[k] for k in LEVEL_KEYS)

    def down_flux(i, v, v_next):
        return gd_r[i] + a_r[i] * (v_next - v)

    def sweep(i, v, v_next, f_prev):
        fd = down_flux(i, v, v_next)
        fr = gr_r[i] + b_r[i] * (right_of(v, steps) - v)
        emit(i, v + w_r[i] * (fd - f_prev + fr - left_of(fr, steps)))
        return fd

    def pair(k, v0, v2, f_prev):
        v1 = e_r[2 * k + 1] + corr[k]
        f_prev = sweep(2 * k, v0, v1, f_prev)
        return sweep(2 * k + 1, v1, v2, f_prev)

    v_first = e_r[0] + corr[0]
    wrapped = chunk_below(v_first)
    v_last = e_r[count - 1] + corr[count // 2 - 1]
    f_prev = chunk_above(down_flux(count - 1, v_last, wrapped))

    def body(k, carry):
        v0, f_prev = carry
        v2 = e_r[2 * k + 2] + corr[k + 1]
        return v2, pair(k, v0, v2, f_prev)

    v0, f_prev = lax.fori_loop(0, count // 2 - 1, body, (v_first, f_prev))
    pair(count // 2 - 1, v0, wrapped, f_prev)


def levels_up(levels, corr, results, shape):
    for depth in range(GRIDS - 1, 0, -1):
        out = results[depth - 1]

        def emit(i, value, out=out):
            out[i] = value

        go_up(levels[depth - 1], corr, depth, shape, emit)
        corr = out
    return corr


def as_levels(refs):
    n = len(LEVEL_KEYS)
    return [dict(zip(LEVEL_KEYS, refs[i : i + n])) for i in range(0, len(refs), n)]


def start_kernel(*refs, shape):
    (swath, coherence, counts, above, below, from_right, from_left) = refs[:7]
    out = refs[7]
    sd_r, sr_r = refs[8:10]
    level_refs = refs[10 : 10 + 6 * GRIDS]
    nat_q, nat_n, rhs, wsum = refs[10 + 6 * GRIDS :]
    rows, ext, tiles = shape.rows, shape.ext_rows, shape.tiles
    level0, *levels = as_levels(level_refs)
    last = dict(est=rhs, w=wsum)

    for t in range(tiles):
        lanes = slice(t * LANE, (t + 1) * LANE)
        nat_q[t, 0:rows, :] = quality_of(swath[:, lanes], coherence[:, lanes])
        nat_n[t, 0:rows, :] = counts[:, lanes].astype(jnp.float32)
        for ref, start in ((below, rows), (above, ext - ROW_HALO)):
            nat_q[t, start : start + ROW_HALO, :] = ref[0:ROW_HALO, lanes]
            nat_n[t, start : start + ROW_HALO, :] = ref[ROW_HALO : 2 * ROW_HALO, lanes]
        if ext > rows + 2 * ROW_HALO:
            gap = slice(rows + ROW_HALO, ext - ROW_HALO)
            nat_q[t, gap, :] = jnp.zeros_like(nat_q[t, gap, :])
            nat_n[t, gap, :] = jnp.zeros_like(nat_n[t, gap, :])
    low = lane_index(LANE) < COL_HALO

    def load(i):
        rows_of = pl.ds(i, SUB, stride=shape.chunk)
        right, left = from_right[rows_of, :], from_left[rows_of, :]
        quality = [nat_q[t, rows_of, :] for t in range(tiles)] + [jnp.where(low, right, left)]
        phase = [nat_n[t, rows_of, :] for t in range(tiles)]
        phase += [pltpu.roll(jnp.where(low, left, right), COL_HALO, 1)]
        return jnp.concatenate(quality, axis=1), jnp.concatenate(phase, axis=1)

    count = shape.chunk

    def down_part(q, n, q_next, n_next):
        a = jnp.minimum(q, q_next)
        sd = wrap_steps(n_next - n)
        return a, sd, -(a * sd)

    def step(i, q, n, q_next, n_next, a_prev, gd_prev):
        a, sd, gd = down_part(q, n, q_next, n_next)
        b = jnp.minimum(q, right_of(q, 1))
        sr = wrap_steps(right_of(n, 1) - n)
        gr = -(b * sr)
        w = relax_weight(a + a_prev + b + left_of(b, 1))
        level0["a"][i] = a
        level0["b"][i] = b
        level0["gd"][i] = gd
        level0["gr"][i] = gr
        level0["w"][i] = w
        level0["est"][i] = w * (gd - gd_prev + gr - left_of(gr, 1))
        sd_r[i] = sd
        sr_r[i] = sr
        return a, gd

    q0, n0 = load(0)
    q_wrap, n_wrap = chunk_below(q0), chunk_below(n0)
    a, _, gd = down_part(*load(count - 1), q_wrap, n_wrap)

    def body(i, carry):
        q, n, a, gd = carry
        q_next, n_next = load(i + 1)
        a, gd = step(i, q, n, q_next, n_next, a, gd)
        return q_next, n_next, a, gd

    q, n, a, gd = lax.fori_loop(0, count - 1, body, (q0, n0, chunk_above(a), chunk_above(gd)))
    step(count - 1, q, n, q_wrap, n_wrap, a, gd)
    levels_down(level0, levels, last, out, shape)


def middle_kernel(*refs, shape):
    gathered, table, sd_r, sr_r = refs[:4]
    old = as_levels(refs[4 : 4 + 6 * GRIDS])
    refs = refs[4 + 6 * GRIDS :]
    out, first = refs[:2]
    level0, *levels = as_levels(refs[2 : 2 + 6 * GRIDS])
    rhs, wsum, corr, *results = refs[2 + 6 * GRIDS :]
    coarse_correction(gathered, table, shape, corr)
    field = levels_up(old[1:], corr, results, shape)

    def emit(i, value):
        first[i] = value

    go_up(old[0], field, 0, shape, emit)

    count = shape.chunk
    a_old, b_old = old[0]["a"], old[0]["b"]

    def down_part(i, v, v_next):
        error = v_next - v - sd_r[i]
        a = a_old[i] / jnp.maximum(jnp.abs(error), error_floor)
        return a, a * error

    def step(i, v, v_next, a_prev, gd_prev):
        a, gd = down_part(i, v, v_next)
        error = right_of(v, 1) - v - sr_r[i]
        b = b_old[i] / jnp.maximum(jnp.abs(error), error_floor)
        gr = b * error
        w = relax_weight(a + a_prev + b + left_of(b, 1))
        level0["a"][i] = a
        level0["b"][i] = b
        level0["gd"][i] = gd
        level0["gr"][i] = gr
        level0["w"][i] = w
        level0["est"][i] = w * (gd - gd_prev + gr - left_of(gr, 1))
        return a, gd

    wrapped = chunk_below(first[0])
    a, gd = down_part(count - 1, first[count - 1], wrapped)

    def body(i, carry):
        v, a, gd = carry
        v_next = first[i + 1]
        return v_next, *step(i, v, v_next, a, gd)

    v, a, gd = lax.fori_loop(0, count - 1, body, (first[0], chunk_above(a), chunk_above(gd)))
    step(count - 1, v, wrapped, a, gd)
    levels_down(level0, levels, dict(est=rhs, w=wsum), out, shape)


def end_kernel(*refs, shape):
    gathered, table, first = refs[:3]
    old = as_levels(refs[3 : 3 + 6 * GRIDS])
    out, nat, corr, *results = refs[3 + 6 * GRIDS :]
    coarse_correction(gathered, table, shape, corr)
    field = levels_up(old[1:], corr, results, shape)

    def emit(i, value):
        value = value + first[i]
        for t in range(shape.tiles):
            nat[t, pl.ds(i, SUB, stride=shape.chunk), :] = value[:, t * LANE : (t + 1) * LANE]

    go_up(old[0], field, 0, shape, emit)
    for t in range(shape.tiles):
        out[:, t * LANE : (t + 1) * LANE] = nat[t, 0 : shape.rows, :]


def dct_table(count):
    freq = np.arange(count)[:, None]
    place = np.arange(count)[None, :]
    table = np.cos(np.pi * (((2 * place + 1) * freq) % (4 * count)) / (2 * count)) * np.sqrt(2.0 / count)
    table[0] *= np.sqrt(0.5)
    return table.astype(np.float32)


def f32(*dims):
    return jax.ShapeDtypeStruct(dims, jnp.float32)


def level_shapes(shape):
    return [f32(shape.slabs(d), SUB, shape.lanes) for d in range(GRIDS) for _ in LEVEL_KEYS]


def vmem(*dims):
    return pltpu.VMEM(dims, jnp.float32)


def exchange(lower, upper, axis):
    count = lax.axis_size(axis)
    up = [(i, i + 1) for i in range(count - 1)]
    down = [(i + 1, i) for i in range(count - 1)]
    return lax.ppermute(upper, axis, up), lax.ppermute(lower, axis, down)


def body(swath, coherence, phase_counts, *, shape):
    params = pltpu.CompilerParams(vmem_limit_bytes=40 * 2**20)
    inputs = (swath, coherence, phase_counts)
    devices = shape.row_count * shape.col_count
    block = f32(devices, SUB, LANE)
    table = jnp.asarray(dct_table(shape.grid_cols))
    coarse_scratch = [vmem(shape.per_chunk, SUB, shape.lanes)] * 2
    result_scratch = [vmem(shape.per_chunk, SUB, shape.lanes)]
    result_scratch += [vmem(shape.slabs(d), SUB, shape.lanes) for d in range(1, GRIDS)]

    strip = f32(2 * ROW_HALO, shape.cols)
    top, bottom = pl.pallas_call(
        row_strip_kernel, out_shape=[strip, strip], compiler_params=params, name="row_strips"
    )(*inputs)
    above, below = exchange(top, bottom, "row")
    strip = f32(shape.ext_rows, LANE)
    first_cols, last_cols = pl.pallas_call(
        functools.partial(col_strip_kernel, shape=shape),
        out_shape=[strip, strip],
        compiler_params=params,
        name="col_strips",
    )(*inputs, above, below)
    from_left, from_right = exchange(first_cols, last_cols, "col")

    field = f32(shape.chunk, SUB, shape.lanes)
    nat = vmem(shape.tiles, shape.ext_rows, LANE)
    block_out, sd, sr, *old = pl.pallas_call(
        functools.partial(start_kernel, shape=shape),
        out_shape=[block, field, field] + level_shapes(shape),
        scratch_shapes=[nat, nat] + coarse_scratch,
        compiler_params=params,
        name="start",
    )(*inputs, above, below, from_right, from_left)
    gathered = lax.all_to_all(block_out, ("row", "col"), split_axis=0, concat_axis=0, tiled=True)
    block_out, first, *old = pl.pallas_call(
        functools.partial(middle_kernel, shape=shape),
        out_shape=[block, field] + level_shapes(shape),
        scratch_shapes=coarse_scratch + result_scratch,
        compiler_params=params,
        name="middle",
    )(gathered, table, sd, sr, *old)
    gathered = lax.all_to_all(block_out, ("row", "col"), split_axis=0, concat_axis=0, tiled=True)
    return pl.pallas_call(
        functools.partial(end_kernel, shape=shape),
        out_shape=f32(shape.rows, shape.cols),
        scratch_shapes=[nat] + result_scratch,
        compiler_params=params,
        name="finish",
    )(gathered, table, first, *old)


def solution(mesh):
    def run(swath, coherence, phase_counts):
        rows, cols = swath.shape
        row_count, col_count = mesh.shape["row"], mesh.shape["col"]
        shape = Shape(rows // row_count, cols // col_count, row_count, col_count)
        return jax.shard_map(
            functools.partial(body, shape=shape),
            mesh=mesh,
            in_specs=(P("row", "col"), P("row", "col"), P("row", "col")),
            out_specs=P("row", "col"),
            check_vma=False,
        )(swath, coherence, phase_counts)

    return run
```

time: 577 us -> 89.9 us (0.16)
  the two profiles are of different devices: /device:TPU:2 before, /device:TPU:0 now
where the time goes in v1:
time: 89.9 us; the launch traced here: 89.5 us
  Pallas kernels  39.4 us (44%)
  blocking collectives  27.6 us (31%)
  starting transfers between devices  9.55 us (11%)
  waiting for transfers between devices  6.61 us (7%)
  local copies, waits for them, and re-layouts  6.32 us (7%)
    all_to_all x2, blocking collectives, body(): lax.all_to_all(block_out, ('row', 'col'), split_axis=0, concat_axis=0, ti...  27.6 us
    pallas_call x1, Pallas kernels, body(): pl.pallas_call(functools.partial(middle_kernel, shape=shape), out_shape=[...  19.9 us
    pallas_call x1, Pallas kernels, body(): pl.pallas_call(functools.partial(start_kernel, shape=shape), out_shape=[b...  12.3 us
    ppermute x4, starting transfers between devices, exchange(): return (lax.ppermute(upper, axis, up), lax.ppermute(lower, axis, down))  9.55 us
    pallas_call x1, Pallas kernels, body(): pl.pallas_call(functools.partial(end_kernel, shape=shape), out_shape=f32(...  6.95 us
    ppermute x4, waiting for transfers between devices, exchange(): return (lax.ppermute(upper, axis, up), lax.ppermute(lower, axis, down))  6.61 us
    unnamed x16, local copies, waits for them, and re-layouts  6.32 us
  transfers between devices with their start and end apart: 4, of which 3 were waited for; matrix products, arithmetic and copies ran while one was open for 0% of the time, Pallas kernels for 0%

profile of v1, /device:TPU:0, one launch (start us, length us, event | category | flops | bytes accessed | tf_op | source)
XLA Modules:
  0.0 89.5 jit_solution(8631455793317426858)
XLA Ops:
  0.0 0.0 copy-start
  0.0 1.0 %copy-done = s32[160,512]{1,0:T(8,128)S(1)} copy-done((s32[160,512]{1,0:T(8,128)S(1)}, s32[160,512]{1,0:T(8,128)}, u32[]{:S(2)}) %copy-start) | copy-done | bytes 327704
  1.0 0.0 copy-start.1
  1.0 1.0 %copy-done.1 = s32[160,512]{1,0:T(8,128)S(1)} copy-done((s32[160,512]{1,0:T(8,128)S(1)}, s32[160,512]{1,0:T(8,128)}, u32[]{:S(2)}) %copy-start.1) | copy-done | bytes 327704
  1.9 0.0 copy-start.2
  1.9 1.0 %copy-done.2 = s32[160,512]{1,0:T(8,128)S(1)} copy-done((s32[160,512]{1,0:T(8,128)S(1)}, s32[160,512]{1,0:T(8,128)}, u32[]{:S(2)}) %copy-start.2) | copy-done | bytes 327704
  3.0 2.4 %collective-permute-start = (f32[96,512]{1,0:T(8,128)S(1)}, f32[96,512]{1,0:T(8,128)S(1)}, u32[]{:S(2)}, u32[]{:S(2)}) collective-permute-start(f32[96,512]{1,0:T(8,128)S(1)} %get-tuple-element.62), channel_id=1, source_target_pairs={{0,8},{8,16},{16,24},{1,9},{9,17},{17,25},{2,10},{10,18},{18,26},{... | collective-permute-start | bytes 589832 | tf_op jit(solution)/shard_map/ppermute | solution.py:490
  5.4 1.3 %collective-permute-start.1 = (f32[96,512]{1,0:T(8,128)S(1)}, f32[96,512]{1,0:T(8,128)S(1)}, u32[]{:S(2)}, u32[]{:S(2)}) collective-permute-start(f32[96,512]{1,0:T(8,128)S(1)} %get-tuple-element.63), channel_id=1, source_target_pairs={{8,0},{16,8},{24,16},{9,1},{17,9},{25,17},{10,2},{18,10},{26,18},{... | collective-permute-start | bytes 589832 | tf_op jit(solution)/shard_map/ppermute | solution.py:490
  6.7 0.0 collective-permute-done.above.refs_3_
  6.7 4.1 %collective-permute-done.1.below.refs_4_ = f32[96,512]{1,0:T(8,128)S(1)} collective-permute-done((f32[96,512]{1,0:T(8,128)S(1)}, f32[96,512]{1,0:T(8,128)S(1)}, u32[]{:S(2)}, u32[]{:S(2)}) %collective-permute-start.1) | collective-permute-done | bytes 196640 | tf_op jit(solution)/shard_map/ppermute | solution.py:490
  10.8 0.1 col_strips.1
  10.9 1.3 %collective-permute-start.2 = (f32[256,128]{1,0:T(8,128)S(1)}, f32[256,128]{1,0:T(8,128)S(1)}, u32[]{:S(2)}, u32[]{:S(2)}) collective-permute-start(f32[256,128]{1,0:T(8,128)S(1)} %get-tuple-element.64), channel_id=1, source_target_pairs={{1,0},{2,1},{3,2},{4,3},{5,4},{6,5},{7,6},{9,8},{10,9},{11,10},{12... | collective-permute-start | bytes 393224 | tf_op jit(solution)/shard_map/ppermute | solution.py:490
  12.2 4.6 %collective-permute-start.3 = (f32[256,128]{1,0:T(8,128)S(1)}, f32[256,128]{1,0:T(8,128)S(1)}, u32[]{:S(2)}, u32[]{:S(2)}) collective-permute-start(f32[256,128]{1,0:T(8,128)S(1)} %get-tuple-element.65), channel_id=1, source_target_pairs={{0,1},{1,2},{2,3},{3,4},{4,5},{5,6},{6,7},{8,9},{9,10},{10,11},{11... | collective-permute-start | bytes 393224 | tf_op jit(solution)/shard_map/ppermute | solution.py:490
  16.8 1.0 %collective-permute-done.2.refs_5_ = f32[256,128]{1,0:T(8,128)S(1)} collective-permute-done((f32[256,128]{1,0:T(8,128)S(1)}, f32[256,128]{1,0:T(8,128)S(1)}, u32[]{:S(2)}, u32[]{:S(2)}) %collective-permute-start.2) | collective-permute-done | bytes 131104 | tf_op jit(solution)/shard_map/ppermute | solution.py:490
  17.8 1.5 %collective-permute-done.3.refs_6_ = f32[256,128]{1,0:T(8,128)S(1)} collective-permute-done((f32[256,128]{1,0:T(8,128)S(1)}, f32[256,128]{1,0:T(8,128)S(1)}, u32[]{:S(2)}, u32[]{:S(2)}) %collective-permute-start.3) | collective-permute-done | bytes 131104 | tf_op jit(solution)/shard_map/ppermute | solution.py:490
  19.3 12.3 %start.1 = (f32[32,8,128]{2,1,0:T(8,128)S(1)}, f32[32,8,640]{2,1,0:T(8,128)S(1)}, f32[32,8,640]{2,1,0:T(8,128)S(1)}, f32[32,8,640]{2,1,0:T(8,128)S(1)}, f32[32,8...) custom-call(s32[160,512]{1,0:T(8,128)S(1)} %copy-done, ...), custom_call_target="tpu_custom_call" | custom-call | tf_op jit(solution)/shard_map/start/pallas_call | solution.py:519
  31.6 0.0 copy-start.4
  31.6 0.8 copy-done.4
  32.5 0.0 copy-start.5
  32.5 0.9 copy-done.5
  33.3 0.0 copy-start.6
  33.3 0.8 copy-done.6
  34.2 0.0 copy-start.7
  34.2 0.8 copy-done.7
  35.0 0.0 copy-start.3
  35.0 17.6 %all_to_all.10.refs_0_ = f32[32,8,128]{2,1,0:T(8,128)S(1)} all-to-all(f32[32,8,128]{2,1,0:T(8,128)S(1)} %get-tuple-element.66), channel_id=1, replica_groups=mesh['row'=4,'col'=8] {'row','col'}, dimensions={0} | all-to-all | bytes 262144 | tf_op jit(solution)/shard_map/all_to_all | solution.py:526
  52.6 0.0 copy-done.3
  52.7 19.9 %middle.1 = (f32[32,8,128]{2,1,0:T(8,128)S(1)}, f32[32,8,640]{2,1,0:T(8,128)S(1)}, f32[32,8,640]{2,1,0:T(8,128)S(1)}, f32[32,8,640]{2,1,0:T(8,128)S(1)}, f32[32,...) custom-call(f32[32,8,128]{2,1,0:T(8,128)S(1)} %all_to_all.10.refs_0_, ...), custom_call_target="tpu_custom_call" | custom-call | tf_op jit(solution)/shard_map/middle/pallas_call | solution.py:527
  72.6 10.0 %all_to_all.11.refs_0_ = f32[32,8,128]{2,1,0:T(8,128)S(1)} all-to-all(f32[32,8,128]{2,1,0:T(8,128)S(1)} %get-tuple-element.93), channel_id=1, replica_groups=mesh['row'=4,'col'=8] {'row','col'}, dimensions={0} | all-to-all | bytes 262144 | tf_op jit(solution)/shard_map/all_to_all | solution.py:534
  82.6 7.0 %finish.1 = f32[160,512]{1,0:T(8,128)} custom-call(f32[32,8,128]{2,1,0:T(8,128)S(1)} %all_to_all.11.refs_0_, f32[256,256]{1,0:T(8,128)S(1)} %copy-done.3, f32[32,8,640]{2,1,0:T(8,128)S(1)} %get-tuple-element.94.refs_2_, f32[32,8,640]{2,1,0:T(8,128)S(1)} %get-tuple-element.95.refs_3_, f32[32,8,640]{2,1,0:T(8,128)S(1)} %get-tuple-element.96.refs_4_, ...), custom_call_target="tpu_custom_call" | custom-call | tf_op jit(solution)/shard_map/finish/pallas_call | solution.py:535
  (1 shorter events, 0.0 us)
Async XLA Ops:
  0.0 1.0 %copy-start = (s32[160,512]{1,0:T(8,128)S(1)}, s32[160,512]{1,0:T(8,128)}, u32[]{:S(2)}) copy-start(s32[160,512]{1,0:T(8,128)} %refs_0_.1) | copy-start | bytes 983044
  1.0 1.0 %copy-start.1 = (s32[160,512]{1,0:T(8,128)S(1)}, s32[160,512]{1,0:T(8,128)}, u32[]{:S(2)}) copy-start(s32[160,512]{1,0:T(8,128)} %refs_1_.3) | copy-start | bytes 983044
  1.9 1.0 %copy-start.2 = (s32[160,512]{1,0:T(8,128)S(1)}, s32[160,512]{1,0:T(8,128)}, u32[]{:S(2)}) copy-start(s32[160,512]{1,0:T(8,128)} %refs_2_.1) | copy-start | bytes 983044
  3.0 3.7 %collective-permute-start = (f32[96,512]{1,0:T(8,128)S(1)}, f32[96,512]{1,0:T(8,128)S(1)}, u32[]{:S(2)}, u32[]{:S(2)}) collective-permute-start(f32[96,512]{1,0:T(8,128)S(1)} %get-tuple-element.62), channel_id=1, source_target_pairs={{0,8},{8,16},{16,24},{1,9},{9,17},{17,25},{2,10},{10,18},{18,26},{... | collective-permute-start | bytes 589832 | tf_op jit(solution)/shard_map/ppermute | solution.py:490
  5.4 5.4 %collective-permute-start.1 = (f32[96,512]{1,0:T(8,128)S(1)}, f32[96,512]{1,0:T(8,128)S(1)}, u32[]{:S(2)}, u32[]{:S(2)}) collective-permute-start(f32[96,512]{1,0:T(8,128)S(1)} %get-tuple-element.63), channel_id=1, source_target_pairs={{8,0},{16,8},{24,16},{9,1},{17,9},{25,17},{10,2},{18,10},{26,18},{... | collective-permute-start | bytes 589832 | tf_op jit(solution)/shard_map/ppermute | solution.py:490
  10.9 6.9 %collective-permute-start.2 = (f32[256,128]{1,0:T(8,128)S(1)}, f32[256,128]{1,0:T(8,128)S(1)}, u32[]{:S(2)}, u32[]{:S(2)}) collective-permute-start(f32[256,128]{1,0:T(8,128)S(1)} %get-tuple-element.64), channel_id=1, source_target_pairs={{1,0},{2,1},{3,2},{4,3},{5,4},{6,5},{7,6},{9,8},{10,9},{11,10},{12... | collective-permute-start | bytes 393224 | tf_op jit(solution)/shard_map/ppermute | solution.py:490
  12.2 7.1 %collective-permute-start.3 = (f32[256,128]{1,0:T(8,128)S(1)}, f32[256,128]{1,0:T(8,128)S(1)}, u32[]{:S(2)}, u32[]{:S(2)}) collective-permute-start(f32[256,128]{1,0:T(8,128)S(1)} %get-tuple-element.65), channel_id=1, source_target_pairs={{0,1},{1,2},{2,3},{3,4},{4,5},{5,6},{6,7},{8,9},{9,10},{10,11},{11... | collective-permute-start | bytes 393224 | tf_op jit(solution)/shard_map/ppermute | solution.py:490
  31.6 0.8 copy-start.4
  32.5 0.9 copy-start.5
  33.3 0.8 copy-start.6
  34.2 0.8 copy-start.7
  35.0 17.6 %copy-start.3 = (f32[256,256]{1,0:T(8,128)S(1)}, f32[256,256]{1,0:T(8,128)}, u32[]{:S(2)}) copy-start(f32[256,256]{1,0:T(8,128)} %constant.2.clone.refs_1_) | copy-start | bytes 786436

commit v2 on v1

v2 whole, which is shorter than its diff:
```python
import functools

import jax
import jax.numpy as jnp
import numpy as np
from jax import lax
from jax.experimental import pallas as pl
from jax.experimental.pallas import tpu as pltpu
from jax.sharding import PartitionSpec as P

GRIDS = 4
LEVELS = 256
NCLASS = 8

damping = 0.8
diag_floor = 0.5
error_floor = 0.5
epsilon = 1e-06
screen_width = 4.0
highest = lax.Precision.HIGHEST

UNROLL = 4
WHOLE = 8

CELL = 2**GRIDS
ROW_HALO = 3 * CELL
COL_HALO = 64
SUB = 8
LANE = 128


class Shape:
    def __init__(self, rows, cols, row_count, col_count):
        self.rows, self.cols = rows, cols
        self.row_count, self.col_count = row_count, col_count
        unit = SUB * CELL
        self.ext_rows = -(-(rows + 2 * ROW_HALO) // unit) * unit
        self.lanes = cols + 2 * COL_HALO
        self.chunk = self.ext_rows // SUB
        self.tiles = cols // LANE
        self.crows, self.ccols = rows // CELL, cols // CELL
        self.per_chunk = self.chunk // CELL
        self.grid_rows = self.crows * row_count
        self.grid_cols = self.ccols * col_count

    def slabs(self, depth):
        return self.chunk >> depth


def quality_of(swath, coherence):
    scaled = coherence.astype(jnp.float32) / (NCLASS - 1)
    return swath.astype(jnp.float32) * (scaled * scaled)


def lane_index(width):
    return lax.broadcasted_iota(jnp.int32, (SUB, width), 1)


def right_of(x, steps):
    return pltpu.roll(x, x.shape[1] - steps, 1)


def left_of(x, steps):
    return pltpu.roll(x, steps, 1)


def chunk_below(x):
    return pltpu.roll(x, SUB - 1, 0)


def chunk_above(x):
    return pltpu.roll(x, 1, 0)


def wrap_steps(difference):
    turns = jnp.floor(difference * (1.0 / LEVELS) + 0.5)
    return (difference - LEVELS * turns) * (2.0 * jnp.pi / LEVELS)


def relax_weight(diagonal):
    return damping / jnp.maximum(diagonal, diag_floor)


def strips_kernel(swath, coherence, counts, quality, phase, top, bottom, s_buf, c_buf, p_buf, sems):
    rows = quality.shape[0]
    copies = [
        pltpu.make_async_copy(src, dst, sems.at[n])
        for n, (src, dst) in enumerate(((swath, s_buf), (coherence, c_buf), (counts, p_buf)))
    ]
    for copy in copies:
        copy.start()
    for copy in copies:
        copy.wait()
    for r in range(0, rows, 2 * SUB):
        here = slice(r, r + 2 * SUB)
        quality[here, :] = quality_of(s_buf[here, :], c_buf[here, :])
        phase[here, :] = p_buf[here, :].astype(jnp.float32)
    for start, out in ((0, top), (rows - ROW_HALO, bottom)):
        here = slice(start, start + ROW_HALO)
        out[0:ROW_HALO, :] = quality[here, :]
        out[ROW_HALO : 2 * ROW_HALO, :] = phase[here, :]


def col_strip_kernel(quality, phase, above, below, first, last, *, shape):
    rows, cols, ext = shape.rows, shape.cols, shape.ext_rows
    low = lax.broadcasted_iota(jnp.int32, (1, LANE), 1) < COL_HALO

    def put(where, q, n):
        first[where, :] = jnp.where(low, q[0], pltpu.roll(n[0], COL_HALO, 1))
        last[where, :] = jnp.where(low, pltpu.roll(n[1], COL_HALO, 1), q[1])

    sides = (slice(0, LANE), slice(cols - LANE, cols))
    put(
        slice(0, rows),
        [quality[:, s] for s in sides],
        [phase[:, s] for s in sides],
    )
    for ref, start in ((below, rows), (above, ext - ROW_HALO)):
        put(
            slice(start, start + ROW_HALO),
            [ref[0:ROW_HALO, s] for s in sides],
            [ref[ROW_HALO : 2 * ROW_HALO, s] for s in sides],
        )
    if ext > rows + 2 * ROW_HALO:
        gap = slice(rows + ROW_HALO, ext - ROW_HALO)
        first[gap, :] = jnp.zeros_like(first[gap, :])
        last[gap, :] = jnp.zeros_like(last[gap, :])


def run(count, step, carry):
    unroll = min(count, UNROLL)
    if count <= WHOLE:
        for i in range(count):
            carry = step(i, carry)
        return carry

    def turn(t, carry):
        for u in range(unroll):
            carry = step(t * unroll + u, carry)
        return carry

    carry = lax.fori_loop(0, count // unroll, turn, carry)
    for i in range(count // unroll * unroll, count):
        carry = step(i, carry)
    return carry


def close(field, count):
    field[count] = chunk_below(field[0])


def put_level(level, i, *values):
    for key, value in zip(LEVEL_KEYS, values):
        level[key][i] = value


def pair_sum(x, steps, odd):
    y = x + right_of(x, steps)
    return jnp.where(odd, left_of(y, steps), y)


def odd_value(x, steps, odd):
    return jnp.where(odd, x, right_of(x, steps))


def go_down(fine, coarse, depth, shape):
    steps = 1 << depth
    count = shape.slabs(depth + 1)
    odd = (lane_index(shape.lanes) & steps) != 0
    a_f, b_f, gd_f, gr_f, v_f = (fine[k] for k in ("a", "b", "gd", "gr", "est"))
    last_level = depth + 1 == GRIDS

    def down_part(k):
        a = a_f[2 * k + 1]
        flux = gd_f[2 * k + 1] + a * (v_f[2 * k + 2] - v_f[2 * k + 1])
        return pair_sum(a, steps, odd), pair_sum(flux, steps, odd)

    def step(k, carry):
        a_prev, gd_prev = carry
        a, gd = down_part(k)
        v0, v1 = v_f[2 * k], v_f[2 * k + 1]
        b0, b1 = b_f[2 * k], b_f[2 * k + 1]
        fr = gr_f[2 * k] + gr_f[2 * k + 1] + b0 * (right_of(v0, steps) - v0) + b1 * (right_of(v1, steps) - v1)
        b = odd_value(b0 + b1, steps, odd)
        gr = odd_value(fr, steps, odd)
        right_side = gd - gd_prev + gr - left_of(gr, 2 * steps)
        if last_level:
            coarse["w"][k] = a + b
            coarse["est"][k] = right_side
        else:
            w = relax_weight(a + a_prev + b + left_of(b, 2 * steps))
            put_level(coarse, k, a, b, gd, gr, w, w * right_side)
        return a, gd

    a, gd = down_part(count - 1)
    run(count, step, (chunk_above(a), chunk_above(gd)))
    if not last_level:
        close(coarse["est"], count)


def lane_select(shape):
    place = lax.broadcasted_iota(jnp.int32, (shape.cols, LANE), 0)
    target = lax.broadcasted_iota(jnp.int32, (shape.cols, LANE), 1)
    return (place == target * CELL).astype(jnp.bfloat16)


def three_parts(x):
    high = x.astype(jnp.bfloat16)
    rest = x - high.astype(jnp.float32)
    middle = rest.astype(jnp.bfloat16)
    low = (rest - middle.astype(jnp.float32)).astype(jnp.bfloat16)
    return high, middle, low


def select_product(x, one_hot):
    n = x.shape[0]
    parts = jnp.concatenate(list(three_parts(x)), axis=0)
    out = jnp.dot(parts, one_hot, preferred_element_type=jnp.float32)
    return out[0:n] + out[n : 2 * n] + out[2 * n : 3 * n]


def publish(coarse, out, shape):
    per = shape.per_chunk
    weights = sum(coarse["w"][j][:, : shape.cols] for j in range(per))
    fields = [coarse["est"][j][:, : shape.cols] for j in range(per)] + [weights]
    packed = select_product(jnp.concatenate(fields, axis=0), lane_select(shape))
    block = packed[0:SUB]
    for j in range(1, per + 1):
        block = block + pltpu.roll(packed[j * SUB : (j + 1) * SUB], j * shape.ccols, 1)
    for device in range(shape.row_count * shape.col_count):
        out[device] = block


LEVEL_KEYS = ("a", "b", "gd", "gr", "w", "est")


def levels_down(level0, levels, last, out, shape):
    chain = [level0] + levels + [last]
    for depth in range(GRIDS):
        go_down(chain[depth], chain[depth + 1], depth, shape)
    publish(last, out, shape)


def coarse_correction(gathered, tables, shape, corr):
    table, forward_x, backward_x, inverse = tables
    rows, cols = shape.row_count, shape.col_count
    per, crows, ccols = shape.per_chunk, shape.crows, shape.ccols
    gr, gc = shape.grid_rows, shape.grid_cols
    group = LANE // ccols
    lane = lane_index(LANE)
    blocks = []
    for j in range(per):
        for r in range(rows):
            pieces = []
            for tile in range(cols // group):
                piece = None
                for g in range(group):
                    x = gathered[r * cols + tile * group + g]
                    shift = ((g - j) * ccols) % LANE
                    x = pltpu.roll(x, shift, 1) if shift else x
                    piece = x if piece is None else jnp.where(lane >= g * ccols, x, piece)
                pieces.append(piece)
            blocks.append(jnp.concatenate(pieces, axis=1))
    strip = jnp.concatenate(blocks, axis=0)

    weights = gathered[0]
    for device in range(1, rows * cols):
        weights = weights + gathered[device]
    sub = lax.broadcasted_iota(jnp.int32, (SUB, LANE), 0)
    own = (sub < crows // per) & (lane >= per * ccols) & (lane < (per + 1) * ccols)
    total = jnp.sum(jnp.where(own, weights, 0.0), keepdims=True)
    count = (gr - 1) * gc + gr * (gc - 1)
    mean = total / count + epsilon

    spectrum = lax.dot_general(strip, table[...], (((1,), (1,)), ((), ())), precision=highest)
    spectrum = jnp.dot(forward_x[...], spectrum, precision=highest)
    spectrum = spectrum * (inverse[...] / mean)
    values = jnp.dot(backward_x[lax.axis_index("row")], spectrum, precision=highest)
    values = jnp.dot(values, table[...], precision=highest)

    def at(dim, size):
        return lax.broadcasted_iota(jnp.int32, size, dim)

    size = (gc, shape.lanes)
    cell = at(1, size) // CELL
    edge = (shape.cols + COL_HALO) // CELL
    cell = jnp.where(cell < edge, cell, cell - shape.lanes // CELL)
    spread = (at(0, size) == cell + lax.axis_index("col") * ccols).astype(jnp.bfloat16)
    values = select_product(values, spread)
    for j in range(per):
        corr[j] = values[j * SUB : (j + 1) * SUB]
    close(corr, per)


def go_up(level, corr, depth, shape, emit):
    steps = 1 << depth
    count = shape.slabs(depth)
    a_r, b_r, gd_r, gr_r, w_r, e_r = (level[k] for k in LEVEL_KEYS)

    def down_flux(i, v, v_next):
        return gd_r[i] + a_r[i] * (v_next - v)

    def sweep(i, v, v_next, f_prev):
        fd = down_flux(i, v, v_next)
        fr = gr_r[i] + b_r[i] * (right_of(v, steps) - v)
        emit(i, v + w_r[i] * (fd - f_prev + fr - left_of(fr, steps)))
        return fd

    def pair(k, carry):
        v0, f_prev = carry
        v1 = e_r[2 * k + 1] + corr[k]
        v2 = e_r[2 * k + 2] + corr[k + 1]
        f_prev = sweep(2 * k, v0, v1, f_prev)
        return v2, sweep(2 * k + 1, v1, v2, f_prev)

    v_last = e_r[count - 1] + corr[count // 2 - 1]
    v_wrap = e_r[count] + corr[count // 2]
    f_prev = chunk_above(down_flux(count - 1, v_last, v_wrap))
    run(count // 2, pair, (e_r[0] + corr[0], f_prev))


def levels_up(levels, corr, results, shape):
    for depth in range(GRIDS - 1, 0, -1):
        out = results[depth - 1]

        def emit(i, value, out=out):
            out[i] = value

        go_up(levels[depth - 1], corr, depth, shape, emit)
        close(out, shape.slabs(depth))
        corr = out
    return corr


def as_levels(refs):
    n = len(LEVEL_KEYS)
    return [dict(zip(LEVEL_KEYS, refs[i : i + n])) for i in range(0, len(refs), n)]


def start_kernel(*refs, shape):
    (quality, counts, above, below, from_right, from_left) = refs[:6]
    out = refs[6]
    sd_r, sr_r = refs[7:9]
    level_refs = refs[9 : 9 + 6 * GRIDS]
    nat_q, nat_n, q_r, n_r, rhs, wsum = refs[9 + 6 * GRIDS :]
    rows, ext, tiles = shape.rows, shape.ext_rows, shape.tiles
    level0, *levels = as_levels(level_refs)

    for t in range(tiles):
        lanes = slice(t * LANE, (t + 1) * LANE)
        nat_q[t, 0:rows, :] = quality[:, lanes]
        nat_n[t, 0:rows, :] = counts[:, lanes]
        for ref, start in ((below, rows), (above, ext - ROW_HALO)):
            nat_q[t, start : start + ROW_HALO, :] = ref[0:ROW_HALO, lanes]
            nat_n[t, start : start + ROW_HALO, :] = ref[ROW_HALO : 2 * ROW_HALO, lanes]
        if ext > rows + 2 * ROW_HALO:
            gap = slice(rows + ROW_HALO, ext - ROW_HALO)
            nat_q[t, gap, :] = jnp.zeros_like(nat_q[t, gap, :])
            nat_n[t, gap, :] = jnp.zeros_like(nat_n[t, gap, :])
    low = lane_index(LANE) < COL_HALO
    count = shape.chunk

    def relay(i, carry):
        rows_of = pl.ds(i, SUB, stride=shape.chunk)
        right, left = from_right[rows_of, :], from_left[rows_of, :]
        q = [nat_q[t, rows_of, :] for t in range(tiles)] + [jnp.where(low, right, left)]
        n = [nat_n[t, rows_of, :] for t in range(tiles)]
        n += [pltpu.roll(jnp.where(low, left, right), COL_HALO, 1)]
        q_r[i] = jnp.concatenate(q, axis=1)
        n_r[i] = jnp.concatenate(n, axis=1)
        return carry

    run(count, relay, 0)
    close(q_r, count)
    close(n_r, count)

    def down_part(i):
        a = jnp.minimum(q_r[i], q_r[i + 1])
        sd = wrap_steps(n_r[i + 1] - n_r[i])
        return a, sd, -(a * sd)

    def step(i, carry):
        a_prev, gd_prev = carry
        a, sd, gd = down_part(i)
        q, n = q_r[i], n_r[i]
        b = jnp.minimum(q, right_of(q, 1))
        sr = wrap_steps(right_of(n, 1) - n)
        gr = -(b * sr)
        w = relax_weight(a + a_prev + b + left_of(b, 1))
        put_level(level0, i, a, b, gd, gr, w, w * (gd - gd_prev + gr - left_of(gr, 1)))
        sd_r[i] = sd
        sr_r[i] = sr
        return a, gd

    a, _, gd = down_part(count - 1)
    run(count, step, (chunk_above(a), chunk_above(gd)))
    close(level0["est"], count)
    levels_down(level0, levels, dict(est=rhs, w=wsum), out, shape)


def middle_kernel(*refs, shape):
    gathered, tables, (sd_r, sr_r) = refs[0], refs[1:5], refs[5:7]
    old = as_levels(refs[7 : 7 + 6 * GRIDS])
    refs = refs[7 + 6 * GRIDS :]
    out, first = refs[:2]
    level0, *levels = as_levels(refs[2 : 2 + 6 * GRIDS])
    rhs, wsum, corr, *results = refs[2 + 6 * GRIDS :]
    coarse_correction(gathered, tables, shape, corr)
    field = levels_up(old[1:], corr, results, shape)

    def emit(i, value):
        first[i] = value

    count = shape.chunk
    go_up(old[0], field, 0, shape, emit)
    close(first, count)
    a_old, b_old = old[0]["a"], old[0]["b"]

    def down_part(i):
        error = first[i + 1] - first[i] - sd_r[i]
        a = a_old[i] / jnp.maximum(jnp.abs(error), error_floor)
        return a, a * error

    def step(i, carry):
        a_prev, gd_prev = carry
        a, gd = down_part(i)
        v = first[i]
        error = right_of(v, 1) - v - sr_r[i]
        b = b_old[i] / jnp.maximum(jnp.abs(error), error_floor)
        gr = b * error
        w = relax_weight(a + a_prev + b + left_of(b, 1))
        put_level(level0, i, a, b, gd, gr, w, w * (gd - gd_prev + gr - left_of(gr, 1)))
        return a, gd

    a, gd = down_part(count - 1)
    run(count, step, (chunk_above(a), chunk_above(gd)))
    close(level0["est"], count)
    levels_down(level0, levels, dict(est=rhs, w=wsum), out, shape)


def end_kernel(*refs, shape):
    gathered, tables, first = refs[0], refs[1:5], refs[5]
    old = as_levels(refs[6 : 6 + 6 * GRIDS])
    out, nat, corr, *results = refs[6 + 6 * GRIDS :]
    coarse_correction(gathered, tables, shape, corr)
    field = levels_up(old[1:], corr, results, shape)

    def emit(i, value):
        value = value + first[i]
        for t in range(shape.tiles):
            nat[t, pl.ds(i, SUB, stride=shape.chunk), :] = value[:, t * LANE : (t + 1) * LANE]

    go_up(old[0], field, 0, shape, emit)
    for t in range(shape.tiles):
        out[:, t * LANE : (t + 1) * LANE] = nat[t, 0 : shape.rows, :]


def dct_table(count):
    freq = np.arange(count)[:, None]
    place = np.arange(count)[None, :]
    table = np.cos(np.pi * (((2 * place + 1) * freq) % (4 * count)) / (2 * count)) * np.sqrt(2.0 / count)
    table[0] *= np.sqrt(0.5)
    return table.astype(np.float32)


def solve_tables(shape):
    gr, gc, per, crows = shape.grid_rows, shape.grid_cols, shape.per_chunk, shape.crows
    table_x = dct_table(gr)
    slab, row, chunk = np.meshgrid(np.arange(per), np.arange(shape.row_count), np.arange(SUB), indexing="ij")
    inside = (chunk < crows // per).ravel()
    place = (row * crows + chunk * per + slab).ravel()
    forward = np.where(inside, table_x[:, np.where(inside, place, 0)], 0)
    slab, chunk = np.meshgrid(np.arange(per), np.arange(SUB), indexing="ij")
    local = (chunk * per + slab).ravel()
    slots = SUB * per
    local = np.where(local < slots - ROW_HALO // CELL, local, local - slots)
    backward = [table_x.T[np.clip(r * crows + local, 0, gr - 1)] for r in range(shape.row_count)]
    lam_x = 2 - 2 * np.cos(np.pi * np.arange(gr) / gr)
    lam_y = 2 - 2 * np.cos(np.pi * np.arange(gc) / gc)
    inverse = 1 / (lam_x[:, None] + lam_y[None, :] + (screen_width / gc) ** 2)
    return [jnp.asarray(x, jnp.float32) for x in (dct_table(gc), forward, np.stack(backward), inverse)]


def f32(*dims):
    return jax.ShapeDtypeStruct(dims, jnp.float32)


def level_shapes(shape):
    return [
        f32(shape.slabs(d) + (key == "est"), SUB, shape.lanes) for d in range(GRIDS) for key in LEVEL_KEYS
    ]


def vmem(*dims):
    return pltpu.VMEM(dims, jnp.float32)


def exchange(lower, upper, axis):
    count = lax.axis_size(axis)
    up = [(i, i + 1) for i in range(count - 1)]
    down = [(i + 1, i) for i in range(count - 1)]
    return lax.ppermute(upper, axis, up), lax.ppermute(lower, axis, down)


def body(swath, coherence, phase_counts, *, shape):
    params = pltpu.CompilerParams(vmem_limit_bytes=16 * 2**20)
    rows, cols = shape.rows, shape.cols
    block = f32(shape.row_count * shape.col_count, SUB, LANE)
    tables = solve_tables(shape)
    coarse_scratch = [vmem(shape.per_chunk, SUB, shape.lanes)] * 2
    result_scratch = [vmem(shape.per_chunk + 1, SUB, shape.lanes)]
    result_scratch += [vmem(shape.slabs(d) + 1, SUB, shape.lanes) for d in range(1, GRIDS)]

    strip = f32(2 * ROW_HALO, cols)
    quality, counts, top, bottom = pl.pallas_call(
        strips_kernel,
        in_specs=[pl.BlockSpec(memory_space=pltpu.HBM)] * 3,
        out_shape=[f32(rows, cols), f32(rows, cols), strip, strip],
        scratch_shapes=[pltpu.VMEM((rows, cols), jnp.int32)] * 3 + [pltpu.SemaphoreType.DMA((3,))],
        compiler_params=params,
        name="row_strips",
    )(swath, coherence, phase_counts)
    above, below = exchange(top, bottom, "row")
    strip = f32(shape.ext_rows, LANE)
    first_cols, last_cols = pl.pallas_call(
        functools.partial(col_strip_kernel, shape=shape),
        out_shape=[strip, strip],
        compiler_params=params,
        name="col_strips",
    )(quality, counts, above, below)
    from_left, from_right = exchange(first_cols, last_cols, "col")

    slabs = (shape.chunk, SUB, shape.lanes)
    more = (shape.chunk + 1, SUB, shape.lanes)
    nat = vmem(shape.tiles, shape.ext_rows, LANE)
    block_out, sd, sr, *old = pl.pallas_call(
        functools.partial(start_kernel, shape=shape),
        out_shape=[block, f32(*slabs), f32(*slabs)] + level_shapes(shape),
        scratch_shapes=[nat, nat, vmem(*more), vmem(*more)] + coarse_scratch,
        compiler_params=params,
        name="start",
    )(quality, counts, above, below, from_right, from_left)
    gathered = lax.all_to_all(block_out, ("row", "col"), split_axis=0, concat_axis=0, tiled=True)
    block_out, first, *old = pl.pallas_call(
        functools.partial(middle_kernel, shape=shape),
        out_shape=[block, f32(*more)] + level_shapes(shape),
        scratch_shapes=coarse_scratch + result_scratch,
        compiler_params=params,
        name="middle",
    )(gathered, *tables, sd, sr, *old)
    gathered = lax.all_to_all(block_out, ("row", "col"), split_axis=0, concat_axis=0, tiled=True)
    return pl.pallas_call(
        functools.partial(end_kernel, shape=shape),
        out_shape=f32(rows, cols),
        scratch_shapes=[nat] + result_scratch,
        compiler_params=params,
        name="finish",
    )(gathered, *tables, first, *old)


def solution(mesh):
    def run(swath, coherence, phase_counts):
        rows, cols = swath.shape
        row_count, col_count = mesh.shape["row"], mesh.shape["col"]
        shape = Shape(rows // row_count, cols // col_count, row_count, col_count)
        return jax.shard_map(
            functools.partial(body, shape=shape),
            mesh=mesh,
            in_specs=(P("row", "col"), P("row", "col"), P("row", "col")),
            out_specs=P("row", "col"),
            check_vma=False,
        )(swath, coherence, phase_counts)

    return run
```

time: 89.9 us -> 67.3 us (0.75)
  Pallas kernels: 39.4 us -> 19.4 us
  local copies, waits for them, and re-layouts: 6.32 us -> 3.7 us
    pallas_call x1, Pallas kernels: 19.9 us -> 8.3 us  [body(): pl.pallas_call(functools.partial(middle_kernel, shape=shape), out_shape=[...]
    pallas_call x1, Pallas kernels: 12.3 us -> 6.71 us  [body(): pl.pallas_call(functools.partial(start_kernel, shape=shape), out_shape=[b...]
    pallas_call x1, Pallas kernels: 6.95 us -> 3.85 us  [body(): pl.pallas_call(functools.partial(end_kernel, shape=shape), out_shape=f32(...]
    unnamed x16 -> x14, local copies, waits for them, and re-layouts: 6.32 us -> 3.7 us
where the time goes in v2:
time: 67.3 us; the launch traced here: 66.9 us
  blocking collectives  27.6 us (41%)
  Pallas kernels  19.4 us (29%)
  starting transfers between devices  9.55 us (14%)
  waiting for transfers between devices  6.61 us (10%)
  local copies, waits for them, and re-layouts  3.7 us (5%)
    all_to_all x2, blocking collectives, body(): lax.all_to_all(block_out, ('row', 'col'), split_axis=0, concat_axis=0, ti...  27.6 us
    ppermute x4, starting transfers between devices, exchange(): return (lax.ppermute(upper, axis, up), lax.ppermute(lower, axis, down))  9.55 us
    pallas_call x1, Pallas kernels, body(): pl.pallas_call(functools.partial(middle_kernel, shape=shape), out_shape=[...  8.3 us
    pallas_call x1, Pallas kernels, body(): pl.pallas_call(functools.partial(start_kernel, shape=shape), out_shape=[b...  6.71 us
    ppermute x4, waiting for transfers between devices, exchange(): return (lax.ppermute(upper, axis, up), lax.ppermute(lower, axis, down))  6.61 us
    pallas_call x1, Pallas kernels, body(): pl.pallas_call(functools.partial(end_kernel, shape=shape), out_shape=f32(...  3.85 us
    unnamed x14, local copies, waits for them, and re-layouts  3.7 us
  transfers between devices with their start and end apart: 4, of which 3 were waited for; matrix products, arithmetic and copies ran while one was open for 0% of the time, Pallas kernels for 0%

profile of v2, /device:TPU:0, one launch (start us, length us, event | category | flops | bytes accessed | tf_op | source)
XLA Modules:
  0.0 66.9 jit_solution(16987792033916146644)
XLA Ops:
  0.0 0.0 copy-start.1
  0.0 1.0 %copy-done.1 = s32[160,512]{1,0:T(8,128)S(1)} copy-done((s32[160,512]{1,0:T(8,128)S(1)}, s32[160,512]{1,0:T(8,128)}, u32[]{:S(2)}) %copy-start.1) | copy-done | bytes 327704
  1.0 0.0 copy-start.2
  1.0 1.0 %copy-done.2 = s32[160,512]{1,0:T(8,128)S(1)} copy-done((s32[160,512]{1,0:T(8,128)S(1)}, s32[160,512]{1,0:T(8,128)}, u32[]{:S(2)}) %copy-start.2) | copy-done | bytes 327704
  1.9 0.0 copy-start.3
  1.9 1.0 %copy-done.3 = s32[160,512]{1,0:T(8,128)S(1)} copy-done((s32[160,512]{1,0:T(8,128)S(1)}, s32[160,512]{1,0:T(8,128)}, u32[]{:S(2)}) %copy-start.3) | copy-done | bytes 327704
  2.9 0.4 row_strips.1
  3.3 2.4 %collective-permute-start = (f32[96,512]{1,0:T(8,128)S(1)}, f32[96,512]{1,0:T(8,128)S(1)}, u32[]{:S(2)}, u32[]{:S(2)}) collective-permute-start(f32[96,512]{1,0:T(8,128)S(1)} %get-tuple-element.66), channel_id=1, source_target_pairs={{0,8},{8,16},{16,24},{1,9},{9,17},{17,25},{2,10},{10,18},{18,26},{... | collective-permute-start | bytes 589832 | tf_op jit(solution)/shard_map/ppermute | solution.py:502
  5.8 1.3 %collective-permute-start.1 = (f32[96,512]{1,0:T(8,128)S(1)}, f32[96,512]{1,0:T(8,128)S(1)}, u32[]{:S(2)}, u32[]{:S(2)}) collective-permute-start(f32[96,512]{1,0:T(8,128)S(1)} %get-tuple-element.67), channel_id=1, source_target_pairs={{8,0},{16,8},{24,16},{9,1},{17,9},{25,17},{10,2},{18,10},{26,18},{... | collective-permute-start | bytes 589832 | tf_op jit(solution)/shard_map/ppermute | solution.py:502
  7.1 0.0 collective-permute-done.above.refs_2_
  7.1 4.1 %collective-permute-done.1.below.refs_3_ = f32[96,512]{1,0:T(8,128)S(1)} collective-permute-done((f32[96,512]{1,0:T(8,128)S(1)}, f32[96,512]{1,0:T(8,128)S(1)}, u32[]{:S(2)}, u32[]{:S(2)}) %collective-permute-start.1) | collective-permute-done | bytes 196640 | tf_op jit(solution)/shard_map/ppermute | solution.py:502
  11.2 0.1 col_strips.1
  11.3 1.3 %collective-permute-start.2 = (f32[256,128]{1,0:T(8,128)S(1)}, f32[256,128]{1,0:T(8,128)S(1)}, u32[]{:S(2)}, u32[]{:S(2)}) collective-permute-start(f32[256,128]{1,0:T(8,128)S(1)} %get-tuple-element.68), channel_id=1, source_target_pairs={{1,0},{2,1},{3,2},{4,3},{5,4},{6,5},{7,6},{9,8},{10,9},{11,10},{12... | collective-permute-start | bytes 393224 | tf_op jit(solution)/shard_map/ppermute | solution.py:502
  12.6 4.6 %collective-permute-start.3 = (f32[256,128]{1,0:T(8,128)S(1)}, f32[256,128]{1,0:T(8,128)S(1)}, u32[]{:S(2)}, u32[]{:S(2)}) collective-permute-start(f32[256,128]{1,0:T(8,128)S(1)} %get-tuple-element.69), channel_id=1, source_target_pairs={{0,1},{1,2},{2,3},{3,4},{4,5},{5,6},{6,7},{8,9},{9,10},{10,11},{11... | collective-permute-start | bytes 393224 | tf_op jit(solution)/shard_map/ppermute | solution.py:502
  17.2 1.0 %collective-permute-done.2.refs_4_ = f32[256,128]{1,0:T(8,128)S(1)} collective-permute-done((f32[256,128]{1,0:T(8,128)S(1)}, f32[256,128]{1,0:T(8,128)S(1)}, u32[]{:S(2)}, u32[]{:S(2)}) %collective-permute-start.2) | collective-permute-done | bytes 131104 | tf_op jit(solution)/shard_map/ppermute | solution.py:502
  18.2 1.5 %collective-permute-done.3.refs_5_ = f32[256,128]{1,0:T(8,128)S(1)} collective-permute-done((f32[256,128]{1,0:T(8,128)S(1)}, f32[256,128]{1,0:T(8,128)S(1)}, u32[]{:S(2)}, u32[]{:S(2)}) %collective-permute-start.3) | collective-permute-done | bytes 131104 | tf_op jit(solution)/shard_map/ppermute | solution.py:502
  19.7 0.0 copy-start.5
  19.7 0.0 copy-start.6
  19.7 6.7 %start.1 = (f32[32,8,128]{2,1,0:T(8,128)S(1)}, f32[32,8,640]{2,1,0:T(8,128)S(1)}, f32[32,8,640]{2,1,0:T(8,128)S(1)}, f32[32,8,640]{2,1,0:T(8,128)S(1)}, f32[32,8...) custom-call(f32[160,512]{1,0:T(8,128)S(1)} %get-tuple-element.64.qua, ...), custom_call_target="tpu_custom_call" | custom-call | tf_op jit(solution)/shard_map/start/pallas_call | solution.py:536
  26.4 0.0 copy-start
  26.4 17.6 %all_to_all.10.refs_0_ = f32[32,8,128]{2,1,0:T(8,128)S(1)} all-to-all(f32[32,8,128]{2,1,0:T(8,128)S(1)} %get-tuple-element.70), channel_id=1, replica_groups=mesh['row'=4,'col'=8] {'row','col'}, dimensions={0} | all-to-all | bytes 262144 | tf_op jit(solution)/shard_map/all_to_all | solution.py:543
  44.0 0.0 copy-start.4
  44.0 0.0 copy-done.5
  44.0 0.0 copy-done.6
  44.0 0.0 copy-done
  44.0 0.8 %copy-done.4 = f32[40,256]{1,0:T(8,128)S(1)} copy-done((f32[40,256]{1,0:T(8,128)S(1)}, f32[40,256]{1,0:T(8,128)}, u32[]{:S(2)}) %copy-start.4) | copy-done | bytes 40984
  44.8 8.3 %middle.1 = (f32[32,8,128]{2,1,0:T(8,128)S(1)}, f32[33,8,640]{2,1,0:T(8,128)S(1)}, f32[32,8,640]{2,1,0:T(8,128)S(1)}, f32[32,8,640]{2,1,0:T(8,128)S(1)}, f32[32,...) custom-call(f32[32,8,128]{2,1,0:T(8,128)S(1)} %all_to_all.10.refs_0_, ...), custom_call_target="tpu_custom_call" | custom-call | tf_op jit(solution)/shard_map/middle/pallas_call | solution.py:544
  53.1 10.0 %all_to_all.11.refs_0_ = f32[32,8,128]{2,1,0:T(8,128)S(1)} all-to-all(f32[32,8,128]{2,1,0:T(8,128)S(1)} %get-tuple-element.97), channel_id=1, replica_groups=mesh['row'=4,'col'=8] {'row','col'}, dimensions={0} | all-to-all | bytes 262144 | tf_op jit(solution)/shard_map/all_to_all | solution.py:551
  63.1 3.9 %finish.1 = f32[160,512]{1,0:T(8,128)} custom-call(f32[32,8,128]{2,1,0:T(8,128)S(1)} %all_to_all.11.refs_0_, f32[256,256]{1,0:T(8,128)S(1)} %copy-done, f32[40,64]{1,0:T(8,128)S(1)} %copy-done.6, f32[4,16,40]{2,1,0:T(8,128)S(1)} %copy-done.5, f32[40,256]{1,0:T(8,128)S(1)} %copy-done.4, f32[33,8,640]{2,1,0:T(8,128)S(1)} %get-tuple-element.98.refs_5_, ...), custom_call_target="tpu_custom_call" | custom-call | tf_op jit(solution)/shard_map/finish/pallas_call | solution.py:552
Async XLA Ops:
  0.0 1.0 %copy-start.1 = (s32[160,512]{1,0:T(8,128)S(1)}, s32[160,512]{1,0:T(8,128)}, u32[]{:S(2)}) copy-start(s32[160,512]{1,0:T(8,128)} %swath.1) | copy-start | bytes 983044
  1.0 1.0 %copy-start.2 = (s32[160,512]{1,0:T(8,128)S(1)}, s32[160,512]{1,0:T(8,128)}, u32[]{:S(2)}) copy-start(s32[160,512]{1,0:T(8,128)} %coherence.1) | copy-start | bytes 983044
  1.9 1.0 %copy-start.3 = (s32[160,512]{1,0:T(8,128)S(1)}, s32[160,512]{1,0:T(8,128)}, u32[]{:S(2)}) copy-start(s32[160,512]{1,0:T(8,128)} %counts.1) | copy-start | bytes 983044
  3.3 3.7 %collective-permute-start = (f32[96,512]{1,0:T(8,128)S(1)}, f32[96,512]{1,0:T(8,128)S(1)}, u32[]{:S(2)}, u32[]{:S(2)}) collective-permute-start(f32[96,512]{1,0:T(8,128)S(1)} %get-tuple-element.66), channel_id=1, source_target_pairs={{0,8},{8,16},{16,24},{1,9},{9,17},{17,25},{2,10},{10,18},{18,26},{... | collective-permute-start | bytes 589832 | tf_op jit(solution)/shard_map/ppermute | solution.py:502
  5.8 5.4 %collective-permute-start.1 = (f32[96,512]{1,0:T(8,128)S(1)}, f32[96,512]{1,0:T(8,128)S(1)}, u32[]{:S(2)}, u32[]{:S(2)}) collective-permute-start(f32[96,512]{1,0:T(8,128)S(1)} %get-tuple-element.67), channel_id=1, source_target_pairs={{8,0},{16,8},{24,16},{9,1},{17,9},{25,17},{10,2},{18,10},{26,18},{... | collective-permute-start | bytes 589832 | tf_op jit(solution)/shard_map/ppermute | solution.py:502
  11.3 6.9 %collective-permute-start.2 = (f32[256,128]{1,0:T(8,128)S(1)}, f32[256,128]{1,0:T(8,128)S(1)}, u32[]{:S(2)}, u32[]{:S(2)}) collective-permute-start(f32[256,128]{1,0:T(8,128)S(1)} %get-tuple-element.68), channel_id=1, source_target_pairs={{1,0},{2,1},{3,2},{4,3},{5,4},{6,5},{7,6},{9,8},{10,9},{11,10},{12... | collective-permute-start | bytes 393224 | tf_op jit(solution)/shard_map/ppermute | solution.py:502
  12.6 7.1 %collective-permute-start.3 = (f32[256,128]{1,0:T(8,128)S(1)}, f32[256,128]{1,0:T(8,128)S(1)}, u32[]{:S(2)}, u32[]{:S(2)}) collective-permute-start(f32[256,128]{1,0:T(8,128)S(1)} %get-tuple-element.69), channel_id=1, source_target_pairs={{0,1},{1,2},{2,3},{3,4},{4,5},{5,6},{6,7},{8,9},{9,10},{10,11},{11... | collective-permute-start | bytes 393224 | tf_op jit(solution)/shard_map/ppermute | solution.py:502
  19.7 24.4 %copy-start.5 = (f32[4,16,40]{2,1,0:T(8,128)S(1)}, f32[4,16,40]{2,1,0:T(8,128)}, u32[]{:S(2)}) copy-start(f32[4,16,40]{2,1,0:T(8,128)} %constant.10.clone.refs_3_) | copy-start | bytes 30724
  19.7 24.4 %copy-start.6 = (f32[40,64]{1,0:T(8,128)S(1)}, f32[40,64]{1,0:T(8,128)}, u32[]{:S(2)}) copy-start(f32[40,64]{1,0:T(8,128)} %constant.9.clone.refs_2_) | copy-start | bytes 30724
  26.4 17.6 %copy-start = (f32[256,256]{1,0:T(8,128)S(1)}, f32[256,256]{1,0:T(8,128)}, u32[]{:S(2)}) copy-start(f32[256,256]{1,0:T(8,128)} %constant.8.clone.refs_1_) | copy-start | bytes 786436
  44.0 0.8 %copy-start.4 = (f32[40,256]{1,0:T(8,128)S(1)}, f32[40,256]{1,0:T(8,128)}, u32[]{:S(2)}) copy-start(f32[40,256]{1,0:T(8,128)} %constant.11.clone.refs_4_) | copy-start | bytes 122884

commit v3 on v2

--- a/solution.py
+++ b/solution.py
@@ -81,8 +81,19 @@
     return damping / jnp.maximum(diagonal, diag_floor)
 
 
-def strips_kernel(swath, coherence, counts, quality, phase, top, bottom, s_buf, c_buf, p_buf, sems):
-    rows = quality.shape[0]
+def position(axis):
+    index, count = lax.axis_index(axis), lax.axis_size(axis)
+    return index % 2 == 0, (index == 0) | (index == count - 1)
+
+
+def aligned(start):
+    return pl.multiple_of(start, SUB)
+
+
+def strips_kernel(
+    swath, coherence, counts, quality, phase, row_even, row_odd, col_even, col_odd, s_buf, c_buf, p_buf, sems
+):
+    rows, cols = quality.shape
     copies = [
         pltpu.make_async_copy(src, dst, sems.at[n])
         for n, (src, dst) in enumerate(((swath, s_buf), (coherence, c_buf), (counts, p_buf)))
@@ -95,36 +106,37 @@
         here = slice(r, r + 2 * SUB)
         quality[here, :] = quality_of(s_buf[here, :], c_buf[here, :])
         phase[here, :] = p_buf[here, :].astype(jnp.float32)
-    for start, out in ((0, top), (rows - ROW_HALO, bottom)):
-        here = slice(start, start + ROW_HALO)
+    even, _ = position("row")
+    bottom = rows - ROW_HALO
+    for out, start in ((row_even, jnp.where(even, bottom, 0)), (row_odd, jnp.where(even, 0, bottom))):
+        here = pl.ds(aligned(start), ROW_HALO)
         out[0:ROW_HALO, :] = quality[here, :]
         out[ROW_HALO : 2 * ROW_HALO, :] = phase[here, :]
-
-
-def col_strip_kernel(quality, phase, above, below, first, last, *, shape):
-    rows, cols, ext = shape.rows, shape.cols, shape.ext_rows
+    even, _ = position("col")
     low = lax.broadcasted_iota(jnp.int32, (1, LANE), 1) < COL_HALO
-
-    def put(where, q, n):
-        first[where, :] = jnp.where(low, q[0], pltpu.roll(n[0], COL_HALO, 1))
-        last[where, :] = jnp.where(low, pltpu.roll(n[1], COL_HALO, 1), q[1])
-
-    sides = (slice(0, LANE), slice(cols - LANE, cols))
-    put(
-        slice(0, rows),
-        [quality[:, s] for s in sides],
-        [phase[:, s] for s in sides],
-    )
-    for ref, start in ((below, rows), (above, ext - ROW_HALO)):
-        put(
-            slice(start, start + ROW_HALO),
-            [ref[0:ROW_HALO, s] for s in sides],
-            [ref[ROW_HALO : 2 * ROW_HALO, s] for s in sides],
-        )
-    if ext > rows + 2 * ROW_HALO:
-        gap = slice(rows + ROW_HALO, ext - ROW_HALO)
-        first[gap, :] = jnp.zeros_like(first[gap, :])
-        last[gap, :] = jnp.zeros_like(last[gap, :])
+    left, right = slice(0, LANE), slice(cols - LANE, cols)
+    first = jnp.where(low, quality[:, left], pltpu.roll(phase[:, left], COL_HALO, 1))
+    last = jnp.where(low, pltpu.roll(phase[:, right], COL_HALO, 1), quality[:, right])
+    col_even[...] = jnp.where(even, last, first)
+    col_odd[...] = jnp.where(even, first, last)
+
+
+def corner_kernel(col_even, col_odd, quality, phase, row_even, row_odd):
+    rows = quality.shape[0]
+    even, at_end = position("col")
+    low = lax.broadcasted_iota(jnp.int32, (1, LANE), 1) < COL_HALO
+    met = col_even[...]
+    other = jnp.where(at_end, 0.0, col_odd[...])
+    right = jnp.where(even, met, other)
+    left = jnp.where(even, other, met)
+    quality[...] = jnp.where(low, right, left)
+    phase[...] = pltpu.roll(jnp.where(low, left, right), COL_HALO, 1)
+    even, _ = position("row")
+    bottom = rows - ROW_HALO
+    for out, start in ((row_even, jnp.where(even, bottom, 0)), (row_odd, jnp.where(even, 0, bottom))):
+        here = pl.ds(aligned(start), ROW_HALO)
+        out[0:ROW_HALO, :] = quality[here, :]
+        out[ROW_HALO : 2 * ROW_HALO, :] = phase[here, :]
 
 
 def run(count, step, carry):
@@ -338,36 +350,36 @@
 
 
 def start_kernel(*refs, shape):
-    (quality, counts, above, below, from_right, from_left) = refs[:6]
-    out = refs[6]
-    sd_r, sr_r = refs[7:9]
-    level_refs = refs[9 : 9 + 6 * GRIDS]
-    nat_q, nat_n, q_r, n_r, rhs, wsum = refs[9 + 6 * GRIDS :]
+    (quality, counts, row_even, row_odd, edge_q, edge_n, corner_even, corner_odd) = refs[:8]
+    out = refs[8]
+    sd_r, sr_r = refs[9:11]
+    level_refs = refs[11 : 11 + 6 * GRIDS]
+    nat_q, nat_n, q_r, n_r, rhs, wsum = refs[11 + 6 * GRIDS :]
     rows, ext, tiles = shape.rows, shape.ext_rows, shape.tiles
     level0, *levels = as_levels(level_refs)
 
-    for t in range(tiles):
-        lanes = slice(t * LANE, (t + 1) * LANE)
-        nat_q[t, 0:rows, :] = quality[:, lanes]
-        nat_n[t, 0:rows, :] = counts[:, lanes]
-        for ref, start in ((below, rows), (above, ext - ROW_HALO)):
-            nat_q[t, start : start + ROW_HALO, :] = ref[0:ROW_HALO, lanes]
-            nat_n[t, start : start + ROW_HALO, :] = ref[ROW_HALO : 2 * ROW_HALO, lanes]
-        if ext > rows + 2 * ROW_HALO:
-            gap = slice(rows + ROW_HALO, ext - ROW_HALO)
-            nat_q[t, gap, :] = jnp.zeros_like(nat_q[t, gap, :])
-            nat_n[t, gap, :] = jnp.zeros_like(nat_n[t, gap, :])
-    low = lane_index(LANE) < COL_HALO
+    even, at_end = position("row")
+    below, above = rows, ext - ROW_HALO
+    met = pl.ds(aligned(jnp.where(even, below, above)), ROW_HALO)
+    other = pl.ds(aligned(jnp.where(even, above, below)), ROW_HALO)
+    for t in range(tiles + 1):
+        lanes = slice(t * LANE, (t + 1) * LANE) if t < tiles else slice(0, LANE)
+        own_q, own_n, from_even, from_odd = (
+            (quality, counts, row_even, row_odd) if t < tiles else (edge_q, edge_n, corner_even, corner_odd)
+        )
+        for nat, own, start in ((nat_q, own_q, 0), (nat_n, own_n, ROW_HALO)):
+            nat[t, 0:rows, :] = own[:, lanes]
+            nat[t, met, :] = from_even[start : start + ROW_HALO, lanes]
+            nat[t, other, :] = jnp.where(at_end, 0.0, from_odd[start : start + ROW_HALO, lanes])
+            if ext > rows + 2 * ROW_HALO:
+                gap = slice(rows + ROW_HALO, ext - ROW_HALO)
+                nat[t, gap, :] = jnp.zeros_like(nat[t, gap, :])
     count = shape.chunk
 
     def relay(i, carry):
         rows_of = pl.ds(i, SUB, stride=shape.chunk)
-        right, left = from_right[rows_of, :], from_left[rows_of, :]
-        q = [nat_q[t, rows_of, :] for t in range(tiles)] + [jnp.where(low, right, left)]
-        n = [nat_n[t, rows_of, :] for t in range(tiles)]
-        n += [pltpu.roll(jnp.where(low, left, right), COL_HALO, 1)]
-        q_r[i] = jnp.concatenate(q, axis=1)
-        n_r[i] = jnp.concatenate(n, axis=1)
+        q_r[i] = jnp.concatenate([nat_q[t, rows_of, :] for t in range(tiles + 1)], axis=1)
+        n_r[i] = jnp.concatenate([nat_n[t, rows_of, :] for t in range(tiles + 1)], axis=1)
         return carry
 
     run(count, relay, 0)
@@ -495,11 +507,26 @@
     return pltpu.VMEM(dims, jnp.float32)
 
 
-def exchange(lower, upper, axis):
-    count = lax.axis_size(axis)
-    up = [(i, i + 1) for i in range(count - 1)]
-    down = [(i + 1, i) for i in range(count - 1)]
-    return lax.ppermute(upper, axis, up), lax.ppermute(lower, axis, down)
+def swap(even_strip, odd_strip, axis):
+    rows, cols = lax.axis_size("row"), lax.axis_size("col")
+    even_pairs, odd_pairs = [], []
+    for r in range(rows):
+        for c in range(cols):
+            here = r * cols + c
+            index, count, step = (r, rows, cols) if axis == "row" else (c, cols, 1)
+            even_pairs.append((here, here + step * ((index ^ 1) - index)))
+            if 0 < index < count - 1:
+                odd_pairs.append((here, here + (step if index % 2 else -step)))
+            else:
+                odd_pairs.append((here, idle_pair(axis, r, c, rows, cols)))
+    both = ("row", "col")
+    return lax.ppermute(even_strip, both, even_pairs), lax.ppermute(odd_strip, both, odd_pairs)
+
+
+def idle_pair(axis, r, c, rows, cols):
+    if axis == "col":
+        return (r ^ 1) * cols + c
+    return (rows - 1 - r) * cols + c
 
 
 def body(swath, coherence, phase_counts, *, shape):
@@ -511,35 +538,36 @@
     result_scratch = [vmem(shape.per_chunk + 1, SUB, shape.lanes)]
     result_scratch += [vmem(shape.slabs(d) + 1, SUB, shape.lanes) for d in range(1, GRIDS)]
 
-    strip = f32(2 * ROW_HALO, cols)
-    quality, counts, top, bottom = pl.pallas_call(
+    strip, edge, corner = f32(2 * ROW_HALO, cols), f32(rows, LANE), f32(2 * ROW_HALO, LANE)
+    quality, counts, row_even, row_odd, col_even, col_odd = pl.pallas_call(
         strips_kernel,
         in_specs=[pl.BlockSpec(memory_space=pltpu.HBM)] * 3,
-        out_shape=[f32(rows, cols), f32(rows, cols), strip, strip],
+        out_shape=[f32(rows, cols), f32(rows, cols), strip, strip, edge, edge],
         scratch_shapes=[pltpu.VMEM((rows, cols), jnp.int32)] * 3 + [pltpu.SemaphoreType.DMA((3,))],
         compiler_params=params,
-        name="row_strips",
-    )(swath, coherence, phase_counts)
-    above, below = exchange(top, bottom, "row")
-    strip = f32(shape.ext_rows, LANE)
-    first_cols, last_cols = pl.pallas_call(
-        functools.partial(col_strip_kernel, shape=shape),
-        out_shape=[strip, strip],
+        name="strips",
+    )(*(pltpu.with_memory_space_constraint(x, pltpu.HBM) for x in (swath, coherence, phase_counts)))
+    row_even, row_odd = swap(row_even, row_odd, "row")
+    col_even, col_odd = swap(col_even, col_odd, "col")
+    edge_q, edge_n, corner_even, corner_odd = pl.pallas_call(
+        corner_kernel,
+        out_shape=[edge, edge, corner, corner],
         compiler_params=params,
-        name="col_strips",
-    )(quality, counts, above, below)
-    from_left, from_right = exchange(first_cols, last_cols, "col")
+        name="corners",
+    )(col_even, col_odd)
+    corner_even, corner_odd = swap(corner_even, corner_odd, "row")
 
     slabs = (shape.chunk, SUB, shape.lanes)
     more = (shape.chunk + 1, SUB, shape.lanes)
     nat = vmem(shape.tiles, shape.ext_rows, LANE)
+    wide = vmem(shape.tiles + 1, shape.ext_rows, LANE)
     block_out, sd, sr, *old = pl.pallas_call(
         functools.partial(start_kernel, shape=shape),
         out_shape=[block, f32(*slabs), f32(*slabs)] + level_shapes(shape),
-        scratch_shapes=[nat, nat, vmem(*more), vmem(*more)] + coarse_scratch,
+        scratch_shapes=[wide, wide, vmem(*more), vmem(*more)] + coarse_scratch,
         compiler_params=params,
         name="start",
-    )(quality, counts, above, below, from_right, from_left)
+    )(quality, counts, row_even, row_odd, edge_q, edge_n, corner_even, corner_odd)
     gathered = lax.all_to_all(block_out, ("row", "col"), split_axis=0, concat_axis=0, tiled=True)
     block_out, first, *old = pl.pallas_call(
         functools.partial(middle_kernel, shape=shape),

time: 67.3 us -> 56.8 us (0.84)
  blocking collectives: 27.6 us -> 23.2 us
  starting transfers between devices: 9.55 us -> 5.34 us
  local copies, waits for them, and re-layouts: 3.7 us -> 0.78 us
  Pallas kernels: 19.4 us -> 20.5 us
    all_to_all x2, blocking collectives: 27.6 us -> 23.2 us  [body(): lax.all_to_all(block_out, ('row', 'col'), split_axis=0, concat_axis=0, ti...]
    ppermute x4 -> x6, starting transfers between devices: 9.55 us -> 5.34 us  [the longest x3 3.2 us: swap(): lax.ppermute(odd_strip, both, odd_pairs)]
    unnamed x14 -> x8, local copies, waits for them, and re-layouts: 3.7 us -> 0.78 us
    pallas_call x1, Pallas kernels: 0.42 us -> 1.37 us  [body(): pl.pallas_call(strips_kernel, in_specs=[pl.BlockSpec(memory_space=pltpu.H...]
    ppermute x4 -> x6, waiting for transfers between devices: 6.61 us -> 6.73 us  [the longest x3 4.36 us: swap(): lax.ppermute(even_strip, both, even_pairs)]
  transfers between devices with their start and end apart: 4 -> 6, of which waited for: 3 -> 3; matrix products, arithmetic and copies ran while one was open for 0% -> 0% of each run, Pallas kernels for 0% -> 0%
where the time goes in v3:
time: 56.8 us; the launch traced here: 56.6 us
  blocking collectives  23.2 us (41%)
  Pallas kernels  20.5 us (36%)
  waiting for transfers between devices  6.73 us (12%)
  starting transfers between devices  5.34 us (9%)
  local copies, waits for them, and re-layouts  0.78 us (1%)
    all_to_all x2, blocking collectives, body(): lax.all_to_all(block_out, ('row', 'col'), split_axis=0, concat_axis=0, ti...  23.2 us
    pallas_call x1, Pallas kernels, body(): pl.pallas_call(functools.partial(middle_kernel, shape=shape), out_shape=[...  8.31 us
    pallas_call x1, Pallas kernels, body(): pl.pallas_call(functools.partial(start_kernel, shape=shape), out_shape=[b...  6.86 us
    ppermute x3, waiting for transfers between devices, swap(): lax.ppermute(even_strip, both, even_pairs)  4.36 us
    pallas_call x1, Pallas kernels, body(): pl.pallas_call(functools.partial(end_kernel, shape=shape), out_shape=f32(...  3.85 us
    ppermute x3, starting transfers between devices, swap(): lax.ppermute(odd_strip, both, odd_pairs)  3.2 us
    ppermute x3, waiting for transfers between devices, swap(): lax.ppermute(odd_strip, both, odd_pairs)  2.37 us
    ppermute x3, starting transfers between devices, swap(): lax.ppermute(even_strip, both, even_pairs)  2.15 us
  transfers between devices with their start and end apart: 6, of which 3 were waited for; matrix products, arithmetic and copies ran while one was open for 0% of the time, Pallas kernels for 0%

profile of v3, /device:TPU:0, one launch (start us, length us, event | category | flops | bytes accessed | tf_op | source)
XLA Modules:
  0.0 56.6 jit_solution(14950543496856870201)
XLA Ops:
  0.0 1.4 %strips.1 = (f32[160,512]{1,0:T(8,128)S(1)}, f32[160,512]{1,0:T(8,128)S(1)}, f32[96,512]{1,0:T(8,128)S(1)}, f32[96,512]{1,0:T(8,128)S(1)}, f32[160,128]{1,0:T(8,128)S(1)}, /*index=5*/f32[160,128]{1,0:T(8,128)S(1)}) custom-call(s32[160,512]{1,0:T(8,128)} %swath.1, s32[160,512]{1,0:T(8,128)} %coherence.1, s32[160,512]{1,0:T(8,128)} %counts.1), custom_call_target="tpu_custom_call" | custom-call | tf_op jit(solution)/shard_map/strips/pallas_call | solution.py:542
  1.4 0.6 collective-permute-start
  1.9 2.6 %collective-permute-start.1 = (f32[96,512]{1,0:T(8,128)S(1)}, f32[96,512]{1,0:T(8,128)S(1)}, u32[]{:S(2)}, u32[]{:S(2)}) collective-permute-start(f32[96,512]{1,0:T(8,128)S(1)} %get-tuple-element.71), channel_id=1, source_target_pairs={{0,24},{1,25},{2,26},{3,27},{4,28},{5,29},{6,30},{7,31},{8,16},{9,... | collective-permute-start | bytes 589832 | tf_op jit(solution)/shard_map/ppermute | solution.py:523
  4.5 1.5 %collective-permute-start.2 = (f32[160,128]{1,0:T(8,128)S(1)}, f32[160,128]{1,0:T(8,128)S(1)}, u32[]{:S(2)}, u32[]{:S(2)}) collective-permute-start(f32[160,128]{1,0:T(8,128)S(1)} %get-tuple-element.72), channel_id=1, source_target_pairs={{0,1},{1,0},{2,3},{3,2},{4,5},{5,4},{6,7},{7,6},{8,9},{9,8},{10,11... | collective-permute-start | bytes 245768 | tf_op jit(solution)/shard_map/ppermute | solution.py:523
  6.0 0.0 collective-permute-start.3
  6.1 3.7 %collective-permute-done.2.col_even = f32[160,128]{1,0:T(8,128)S(1)} collective-permute-done((f32[160,128]{1,0:T(8,128)S(1)}, f32[160,128]{1,0:T(8,128)S(1)}, u32[]{:S(2)}, u32[]{:S(2)}) %collective-permute-start.2) | collective-permute-done | bytes 81952 | tf_op jit(solution)/shard_map/ppermute | solution.py:523
  9.8 0.0 collective-permute-done.3.col_odd
  9.8 0.1 corners.1
  9.9 0.1 collective-permute-start.4
  10.0 0.6 %collective-permute-start.5 = (f32[96,128]{1,0:T(8,128)S(1)}, f32[96,128]{1,0:T(8,128)S(1)}, u32[]{:S(2)}, u32[]{:S(2)}) collective-permute-start(f32[96,128]{1,0:T(8,128)S(1)} %get-tuple-element.77), channel_id=1, source_target_pairs={{0,24},{1,25},{2,26},{3,27},{4,28},{5,29},{6,30},{7,31},{8,16},{9,... | collective-permute-start | bytes 147464 | tf_op jit(solution)/shard_map/ppermute | solution.py:523
  10.6 0.6 %collective-permute-done.4.refs_6_ = f32[96,128]{1,0:T(8,128)S(1)} collective-permute-done((f32[96,128]{1,0:T(8,128)S(1)}, f32[96,128]{1,0:T(8,128)S(1)}, u32[]{:S(2)}, u32[]{:S(2)}) %collective-permute-start.4) | collective-permute-done | bytes 49184 | tf_op jit(solution)/shard_map/ppermute | solution.py:523
  11.2 2.4 %collective-permute-done.5.refs_7_ = f32[96,128]{1,0:T(8,128)S(1)} collective-permute-done((f32[96,128]{1,0:T(8,128)S(1)}, f32[96,128]{1,0:T(8,128)S(1)}, u32[]{:S(2)}, u32[]{:S(2)}) %collective-permute-start.5) | collective-permute-done | bytes 49184 | tf_op jit(solution)/shard_map/ppermute | solution.py:523
  13.6 0.0 collective-permute-done.refs_2_
  13.6 0.0 collective-permute-done.1.refs_3_
  13.6 0.0 copy-start.2
  13.6 0.0 copy-start.3
  13.6 6.9 %start.1 = (f32[32,8,128]{2,1,0:T(8,128)S(1)}, f32[32,8,640]{2,1,0:T(8,128)S(1)}, f32[32,8,640]{2,1,0:T(8,128)S(1)}, f32[32,8,640]{2,1,0:T(8,128)S(1)}, f32[32,8...) custom-call(f32[160,512]{1,0:T(8,128)S(1)} %get-tuple-element.68.ref, ...), custom_call_target="tpu_custom_call" | custom-call | tf_op jit(solution)/shard_map/start/pallas_call | solution.py:564
  20.4 0.0 copy-start
  20.5 13.2 %all_to_all.10.refs_0_ = f32[32,8,128]{2,1,0:T(8,128)S(1)} all-to-all(f32[32,8,128]{2,1,0:T(8,128)S(1)} %get-tuple-element.78), channel_id=1, replica_groups=mesh['row'=4,'col'=8] {'row','col'}, dimensions={0} | all-to-all | bytes 262144 | tf_op jit(solution)/shard_map/all_to_all | solution.py:571
  33.7 0.0 copy-start.1
  33.7 0.0 copy-done.2
  33.7 0.0 copy-done.3
  33.7 0.0 copy-done
  33.7 0.8 %copy-done.1 = f32[40,256]{1,0:T(8,128)S(1)} copy-done((f32[40,256]{1,0:T(8,128)S(1)}, f32[40,256]{1,0:T(8,128)}, u32[]{:S(2)}) %copy-start.1) | copy-done | bytes 40984
  34.4 8.3 %middle.1 = (f32[32,8,128]{2,1,0:T(8,128)S(1)}, f32[33,8,640]{2,1,0:T(8,128)S(1)}, f32[32,8,640]{2,1,0:T(8,128)S(1)}, f32[32,8,640]{2,1,0:T(8,128)S(1)}, f32[32,...) custom-call(f32[32,8,128]{2,1,0:T(8,128)S(1)} %all_to_all.10.refs_0_, ...), custom_call_target="tpu_custom_call" | custom-call | tf_op jit(solution)/shard_map/middle/pallas_call | solution.py:572
  42.8 10.0 %all_to_all.11.refs_0_ = f32[32,8,128]{2,1,0:T(8,128)S(1)} all-to-all(f32[32,8,128]{2,1,0:T(8,128)S(1)} %get-tuple-element.105), channel_id=1, replica_groups=mesh['row'=4,'col'=8] {'row','col'}, dimensions={0} | all-to-all | bytes 262144 | tf_op jit(solution)/shard_map/all_to_all | solution.py:579
  52.7 3.9 %finish.1 = f32[160,512]{1,0:T(8,128)} custom-call(f32[32,8,128]{2,1,0:T(8,128)S(1)} %all_to_all.11.refs_0_, f32[256,256]{1,0:T(8,128)S(1)} %copy-done, f32[40,64]{1,0:T(8,128)S(1)} %copy-done.3, f32[4,16,40]{2,1,0:T(8,128)S(1)} %copy-done.2, f32[40,256]{1,0:T(8,128)S(1)} %copy-done.1, f32[33,8,640]{2,1,0:T(8,128)S(1)} %get-tuple-element.106.refs_5_, ...), custom_call_target="tpu_custom_call" | custom-call | tf_op jit(solution)/shard_map/finish/pallas_call | solution.py:580
Async XLA Ops:
  1.4 12.2 %collective-permute-start = (f32[96,512]{1,0:T(8,128)S(1)}, f32[96,512]{1,0:T(8,128)S(1)}, u32[]{:S(2)}, u32[]{:S(2)}) collective-permute-start(f32[96,512]{1,0:T(8,128)S(1)} %get-tuple-element.70), channel_id=1, source_target_pairs={{0,8},{1,9},{2,10},{3,11},{4,12},{5,13},{6,14},{7,15},{8,0},{9,1},... | collective-permute-start | bytes 589832 | tf_op jit(solution)/shard_map/ppermute | solution.py:523
  1.9 11.6 %collective-permute-start.1 = (f32[96,512]{1,0:T(8,128)S(1)}, f32[96,512]{1,0:T(8,128)S(1)}, u32[]{:S(2)}, u32[]{:S(2)}) collective-permute-start(f32[96,512]{1,0:T(8,128)S(1)} %get-tuple-element.71), channel_id=1, source_target_pairs={{0,24},{1,25},{2,26},{3,27},{4,28},{5,29},{6,30},{7,31},{8,16},{9,... | collective-permute-start | bytes 589832 | tf_op jit(solution)/shard_map/ppermute | solution.py:523
  4.5 5.3 %collective-permute-start.2 = (f32[160,128]{1,0:T(8,128)S(1)}, f32[160,128]{1,0:T(8,128)S(1)}, u32[]{:S(2)}, u32[]{:S(2)}) collective-permute-start(f32[160,128]{1,0:T(8,128)S(1)} %get-tuple-element.72), channel_id=1, source_target_pairs={{0,1},{1,0},{2,3},{3,2},{4,5},{5,4},{6,7},{7,6},{8,9},{9,8},{10,11... | collective-permute-start | bytes 245768 | tf_op jit(solution)/shard_map/ppermute | solution.py:523
  6.0 3.8 %collective-permute-start.3 = (f32[160,128]{1,0:T(8,128)S(1)}, f32[160,128]{1,0:T(8,128)S(1)}, u32[]{:S(2)}, u32[]{:S(2)}) collective-permute-start(f32[160,128]{1,0:T(8,128)S(1)} %get-tuple-element.73), channel_id=1, source_target_pairs={{0,8},{1,2},{2,1},{3,4},{4,3},{5,6},{6,5},{7,15},{8,0},{9,10},{10,... | collective-permute-start | bytes 245768 | tf_op jit(solution)/shard_map/ppermute | solution.py:523
  9.9 1.3 %collective-permute-start.4 = (f32[96,128]{1,0:T(8,128)S(1)}, f32[96,128]{1,0:T(8,128)S(1)}, u32[]{:S(2)}, u32[]{:S(2)}) collective-permute-start(f32[96,128]{1,0:T(8,128)S(1)} %get-tuple-element.76), channel_id=1, source_target_pairs={{0,8},{1,9},{2,10},{3,11},{4,12},{5,13},{6,14},{7,15},{8,0},{9,1},... | collective-permute-start | bytes 147464 | tf_op jit(solution)/shard_map/ppermute | solution.py:523
  10.0 3.6 %collective-permute-start.5 = (f32[96,128]{1,0:T(8,128)S(1)}, f32[96,128]{1,0:T(8,128)S(1)}, u32[]{:S(2)}, u32[]{:S(2)}) collective-permute-start(f32[96,128]{1,0:T(8,128)S(1)} %get-tuple-element.77), channel_id=1, source_target_pairs={{0,24},{1,25},{2,26},{3,27},{4,28},{5,29},{6,30},{7,31},{8,16},{9,... | collective-permute-start | bytes 147464 | tf_op jit(solution)/shard_map/ppermute | solution.py:523
  13.6 20.1 %copy-start.2 = (f32[4,16,40]{2,1,0:T(8,128)S(1)}, f32[4,16,40]{2,1,0:T(8,128)}, u32[]{:S(2)}) copy-start(f32[4,16,40]{2,1,0:T(8,128)} %constant.10.clone.refs_3_) | copy-start | bytes 30724
  13.6 20.1 %copy-start.3 = (f32[40,64]{1,0:T(8,128)S(1)}, f32[40,64]{1,0:T(8,128)}, u32[]{:S(2)}) copy-start(f32[40,64]{1,0:T(8,128)} %constant.9.clone.refs_2_) | copy-start | bytes 30724
  20.4 13.2 %copy-start = (f32[256,256]{1,0:T(8,128)S(1)}, f32[256,256]{1,0:T(8,128)}, u32[]{:S(2)}) copy-start(f32[256,256]{1,0:T(8,128)} %constant.8.clone.refs_1_) | copy-start | bytes 786436
  33.7 0.8 %copy-start.1 = (f32[40,256]{1,0:T(8,128)S(1)}, f32[40,256]{1,0:T(8,128)}, u32[]{:S(2)}) copy-start(f32[40,256]{1,0:T(8,128)} %constant.11.clone.refs_4_) | copy-start | bytes 122884

commit v4 on v3

v4 whole, which is shorter than its diff:
```python
import functools

import jax
import jax.numpy as jnp
import numpy as np
from jax import lax
from jax.experimental import pallas as pl
from jax.experimental.pallas import tpu as pltpu
from jax.sharding import PartitionSpec as P

GRIDS = 4
LEVELS = 256
NCLASS = 8

damping = 0.8
diag_floor = 0.5
error_floor = 0.5
epsilon = 1e-06
screen_width = 4.0
highest = lax.Precision.HIGHEST

UNROLL_TOP = 4
UNROLL_DOWN = 4
UNROLL_UP = 4
WHOLE = 8

CELL = 2**GRIDS
ROW_HALO = 3 * CELL
COL_HALO = 64
SUB = 8
LANE = 128


class Shape:
    def __init__(self, rows, cols, row_count, col_count):
        self.rows, self.cols = rows, cols
        self.row_count, self.col_count = row_count, col_count
        unit = SUB * CELL
        self.ext_rows = -(-(rows + 2 * ROW_HALO) // unit) * unit
        self.lanes = cols + 2 * COL_HALO
        self.chunk = self.ext_rows // SUB
        self.tiles = cols // LANE
        self.crows, self.ccols = rows // CELL, cols // CELL
        self.per_chunk = self.chunk // CELL
        self.grid_rows = self.crows * row_count
        self.grid_cols = self.ccols * col_count
        self.group = LANE // self.ccols
        self.block_rows = SUB * self.per_chunk // self.group
        self.fold = SUB // self.block_rows
        assert self.group % self.per_chunk == 0 and self.crows <= self.group * (self.block_rows - 1)
        assert col_count % (self.fold * self.group) == 0 and self.crows % self.per_chunk == 0

    def slabs(self, depth):
        return self.chunk >> depth


def quality_of(swath, coherence):
    scaled = coherence.astype(jnp.float32) / (NCLASS - 1)
    return swath.astype(jnp.float32) * (scaled * scaled)


def lane_index(width):
    return lax.broadcasted_iota(jnp.int32, (SUB, width), 1)


def right_of(x, steps):
    return pltpu.roll(x, x.shape[1] - steps, 1)


def left_of(x, steps):
    return pltpu.roll(x, steps, 1)


def chunk_below(x):
    return pltpu.roll(x, SUB - 1, 0)


def chunk_above(x):
    return pltpu.roll(x, 1, 0)


def wrap_steps(difference):
    turns = jnp.floor(difference * (1.0 / LEVELS) + 0.5)
    return (difference - LEVELS * turns) * (2.0 * jnp.pi / LEVELS)


def relax_weight(diagonal):
    return damping / jnp.maximum(diagonal, diag_floor)


def position(axis):
    index, count = lax.axis_index(axis), lax.axis_size(axis)
    return index % 2 == 0, (index == 0) | (index == count - 1)


def aligned(start):
    return pl.multiple_of(start, SUB)


def strips_kernel(
    swath, coherence, counts, quality, phase, row_even, row_odd, col_even, col_odd, s_buf, c_buf, p_buf, sems
):
    rows, cols = quality.shape
    copies = [
        pltpu.make_async_copy(src, dst, sems.at[n])
        for n, (src, dst) in enumerate(((swath, s_buf), (coherence, c_buf), (counts, p_buf)))
    ]
    for copy in copies:
        copy.start()
    for copy in copies:
        copy.wait()
    for r in range(0, rows, 2 * SUB):
        here = slice(r, r + 2 * SUB)
        quality[here, :] = quality_of(s_buf[here, :], c_buf[here, :])
        phase[here, :] = p_buf[here, :].astype(jnp.float32)
    even, _ = position("row")
    bottom = rows - ROW_HALO
    for out, start in ((row_even, jnp.where(even, bottom, 0)), (row_odd, jnp.where(even, 0, bottom))):
        here = pl.ds(aligned(start), ROW_HALO)
        out[0:ROW_HALO, :] = quality[here, :]
        out[ROW_HALO : 2 * ROW_HALO, :] = phase[here, :]
    even, _ = position("col")
    low = lax.broadcasted_iota(jnp.int32, (1, LANE), 1) < COL_HALO
    left, right = slice(0, LANE), slice(cols - LANE, cols)
    first = jnp.where(low, quality[:, left], pltpu.roll(phase[:, left], COL_HALO, 1))
    last = jnp.where(low, pltpu.roll(phase[:, right], COL_HALO, 1), quality[:, right])
    col_even[...] = jnp.where(even, last, first)
    col_odd[...] = jnp.where(even, first, last)


def corner_kernel(col_even, col_odd, quality, phase, row_even, row_odd):
    rows = quality.shape[0]
    even, at_end = position("col")
    low = lax.broadcasted_iota(jnp.int32, (1, LANE), 1) < COL_HALO
    met = col_even[...]
    other = jnp.where(at_end, 0.0, col_odd[...])
    right = jnp.where(even, met, other)
    left = jnp.where(even, other, met)
    quality[...] = jnp.where(low, right, left)
    phase[...] = pltpu.roll(jnp.where(low, left, right), COL_HALO, 1)
    even, _ = position("row")
    bottom = rows - ROW_HALO
    for out, start in ((row_even, jnp.where(even, bottom, 0)), (row_odd, jnp.where(even, 0, bottom))):
        here = pl.ds(aligned(start), ROW_HALO)
        out[0:ROW_HALO, :] = quality[here, :]
        out[ROW_HALO : 2 * ROW_HALO, :] = phase[here, :]


class Stores:
    def __init__(self):
        self.waiting = []

    def put(self, ref, index, value):
        self.waiting.append((ref, index, value))

    def flush(self):
        for ref, index, value in self.waiting:
            ref[index] = value
        self.waiting = []


def run(count, step, carry, unroll):
    unroll = min(count, unroll)

    def turn(t, carry):
        stores = Stores()
        for u in range(unroll):
            carry = step(t * unroll + u, carry, stores.put)
        stores.flush()
        return carry

    turns = count // unroll
    if count <= WHOLE:
        for t in range(turns):
            carry = turn(t, carry)
    else:
        carry = lax.fori_loop(0, turns, turn, carry)
    assert turns * unroll == count
    return carry


def close(field, count):
    field[count] = chunk_below(field[0])


def put_level(put, level, i, *values):
    for key, value in zip(TOP_KEYS, values):
        put(level[key], i, value)


def spread(x, steps):
    return jnp.where((lane_index(x.shape[1]) & steps) != 0, x, right_of(x, steps))


def go_down(fine, coarse, depth, shape):
    steps = 1 << depth
    count = shape.slabs(depth + 1)
    a_f, b_f, gd_f, gr_f, v_f = (fine[k] for k in ("a", "b", "gd", "gr", "est"))
    last_level = depth + 1 == GRIDS

    def down_part(k):
        a = a_f[2 * k + 1]
        flux = gd_f[2 * k + 1] + a * (v_f[2 * k + 2] - v_f[2 * k + 1])
        return a + left_of(a, steps), flux + left_of(flux, steps)

    def step(k, carry, put):
        a_prev, gd_prev = carry
        a, gd = down_part(k)
        v0, v1 = v_f[2 * k], v_f[2 * k + 1]
        b0, b1 = b_f[2 * k], b_f[2 * k + 1]
        gr = gr_f[2 * k] + gr_f[2 * k + 1] + b0 * (right_of(v0, steps) - v0) + b1 * (right_of(v1, steps) - v1)
        b = b0 + b1
        right_side = gd - gd_prev + gr - left_of(gr, 2 * steps)
        if last_level:
            put(coarse["w"], k, a + b)
            put(coarse["est"], k, right_side)
        else:
            w = relax_weight(a + a_prev + b + left_of(b, 2 * steps))
            put_level(put, coarse, k, a, b, gd, gr, w, w * right_side)
        return a, gd

    a, gd = down_part(count - 1)
    run(count, step, (chunk_above(a), chunk_above(gd)), UNROLL_DOWN)
    if not last_level:
        close(coarse["est"], count)


def lane_select(shape):
    place = lax.broadcasted_iota(jnp.int32, (shape.cols, LANE), 0)
    target = lax.broadcasted_iota(jnp.int32, (shape.cols, LANE), 1)
    return (place == target * CELL + CELL - 1).astype(jnp.bfloat16)


def parts_of(x, count):
    parts = []
    for _ in range(count):
        part = x.astype(jnp.bfloat16)
        x = x - part.astype(jnp.float32)
        parts.append(part)
    return parts


def rows_of_parts(x, count):
    return jnp.concatenate(parts_of(x, count), axis=0)


def product(left, right, count):
    n = left.shape[0] // count
    out = None
    for p in range(count):
        wide = jnp.dot(left[0 : (count - p) * n], right[p], preferred_element_type=jnp.float32)
        for q in reversed(range(count - p)):
            piece = wide[q * n : (q + 1) * n]
            out = piece if out is None else out + piece
    return out


def select_product(x, one_hot, count):
    n = x.shape[0]
    out = jnp.dot(rows_of_parts(x, count), one_hot, preferred_element_type=jnp.float32)
    return sum(out[p * n : (p + 1) * n] for p in range(count))


def publish(coarse, pack, out, shape):
    per, chunks = shape.per_chunk, shape.crows // shape.per_chunk
    weights = sum(coarse["w"][j][:, : shape.cols] for j in range(per))
    fields = [coarse["est"][j][:, : shape.cols] for j in range(per)] + [weights]
    packed = select_product(jnp.concatenate(fields, axis=0), lane_select(shape), 3)
    sub = lax.broadcasted_iota(jnp.int32, (SUB, LANE), 0)
    total = jnp.sum(jnp.where(sub < chunks, packed[per * SUB :], 0.0), axis=0, keepdims=True)
    block = None
    for j in range(per):
        pack[j] = packed[j * SUB : (j + 1) * SUB]
    stride = shape.group // per
    for t in range(stride):
        for j in range(per):
            shift = (per * t + j) * shape.ccols
            x = pack[j, pl.ds(t, shape.block_rows, stride=stride), :]
            x = pltpu.roll(x, shift, 1) if shift else x
            block = x if block is None else block + x
    row = lax.broadcasted_iota(jnp.int32, block.shape, 0)
    block = jnp.where(row == shape.block_rows - 1, total, block)
    for device in range(shape.row_count * shape.col_count):
        out[device] = block


LEVEL_KEYS = ("a", "b", "gd", "gr", "w", "est")
TOP_KEYS = LEVEL_KEYS + ("bl", "gl")
LEVEL_REFS = len(TOP_KEYS) + (GRIDS - 1) * len(LEVEL_KEYS)


def levels_down(level0, levels, last, pack, out, shape):
    chain = [level0] + levels + [last]
    for depth in range(GRIDS):
        go_down(chain[depth], chain[depth + 1], depth, shape)
    publish(last, pack, out, shape)


def coarse_correction(gathered, tables, shape, corr):
    transforms, row_tables, inverse = tables
    rows, cols = shape.row_count, shape.col_count // shape.fold
    per, ccols, group = shape.per_chunk, shape.ccols, shape.group
    gr, gc = shape.grid_rows, shape.grid_cols
    lane = lane_index(LANE)
    blocks = []
    for g in range(group):
        for r in range(rows):
            pieces = []
            for tile in range(cols // group):
                piece = None
                for place in range(group):
                    x = gathered[r * cols + tile * group + place]
                    shift = ((place - g) * ccols) % LANE
                    x = pltpu.roll(x, shift, 1) if shift else x
                    piece = x if piece is None else jnp.where(lane >= place * ccols, x, piece)
                pieces.append(piece)
            blocks.append(jnp.concatenate(pieces, axis=1))
    strip = jnp.concatenate(blocks, axis=0)

    weights = gathered[0]
    for device in range(1, rows * cols):
        weights = weights + gathered[device]
    sub = lax.broadcasted_iota(jnp.int32, (SUB, LANE), 0)
    here = (sub % shape.block_rows == shape.block_rows - 1) & (lane < ccols)
    total = jnp.sum(jnp.where(here, weights, 0.0), keepdims=True)
    count = (gr - 1) * gc + gr * (gc - 1)
    mean = total / count + epsilon

    forward = 3 * shape.fold * gr
    spectrum = product(row_tables[0:forward, : strip.shape[0]], parts_of(strip, 3), 3)
    spectrum = jnp.concatenate([spectrum[f * gr : (f + 1) * gr] for f in range(shape.fold)], axis=1)
    spectrum = product(rows_of_parts(spectrum, 3), [transforms[p * gc : (p + 1) * gc] for p in range(3)], 3)
    spectrum = spectrum * (inverse[...] * (1.0 / mean))
    slots = SUB * per
    start = pl.multiple_of(forward + lax.axis_index("row") * 2 * slots, 2 * slots)
    backward = row_tables[pl.ds(start, 2 * slots), :][:, :gr]
    values = product(backward, parts_of(spectrum, 2), 2)
    values = product(rows_of_parts(values, 2), [transforms[p * gc : (p + 1) * gc] for p in (3, 4)], 2)

    def at(dim, size):
        return lax.broadcasted_iota(jnp.int32, size, dim)

    size = (gc, shape.lanes)
    cell = at(1, size) // CELL
    edge = (shape.cols + COL_HALO) // CELL
    cell = jnp.where(cell < edge, cell, cell - shape.lanes // CELL)
    to_lanes = (at(0, size) == cell + lax.axis_index("col") * ccols).astype(jnp.bfloat16)
    values = select_product(values, to_lanes, 2)
    for j in range(per):
        corr[j] = values[j * SUB : (j + 1) * SUB]
    close(corr, per)


def go_up(level, corr, depth, shape, emit):
    steps = 1 << depth
    count = shape.slabs(depth)
    a_r, b_r, gd_r, gr_r, w_r, e_r = (level[k] for k in LEVEL_KEYS)
    top = depth == 0

    def down_flux(i, v, v_next):
        return gd_r[i] + a_r[i] * (v_next - v)

    def sweep(i, v, v_next, f_prev, put):
        fd = down_flux(i, v, v_next)
        fr = gr_r[i] + b_r[i] * (right_of(v, steps) - v)
        fl = level["gl"][i] + level["bl"][i] * (v - left_of(v, 1)) if top else left_of(fr, steps)
        emit(put, i, v + w_r[i] * (fd - f_prev + fr - fl))
        return fd

    def pair(k, carry, put):
        v0, f_prev = carry
        v1 = e_r[2 * k + 1] + corr[k]
        v2 = e_r[2 * k + 2] + corr[k + 1]
        f_prev = sweep(2 * k, v0, v1, f_prev, put)
        return v2, sweep(2 * k + 1, v1, v2, f_prev, put)

    v_last = e_r[count - 1] + corr[count // 2 - 1]
    v_wrap = e_r[count] + corr[count // 2]
    f_prev = chunk_above(down_flux(count - 1, v_last, v_wrap))
    run(count // 2, pair, (e_r[0] + corr[0], f_prev), UNROLL_UP)


def levels_up(levels, corr, results, shape):
    for depth in range(GRIDS - 1, 0, -1):
        out = results[depth - 1]

        def emit(put, i, value, out=out, depth=depth):
            put(out, i, spread(value, 1 << (depth - 1)))

        go_up(levels[depth - 1], corr, depth, shape, emit)
        close(out, shape.slabs(depth))
        corr = out
    return corr


def as_levels(refs):
    n, top = len(LEVEL_KEYS), len(TOP_KEYS)
    rest = [dict(zip(LEVEL_KEYS, refs[i : i + n])) for i in range(top, len(refs), n)]
    return [dict(zip(TOP_KEYS, refs[:top]))] + rest


def start_kernel(*refs, shape):
    (quality, counts, row_even, row_odd, edge_q, edge_n, corner_even, corner_odd) = refs[:8]
    refs = refs[9:]
    out = refs[0]
    sd_r, sr_r, sl_r = refs[1:4]
    level_refs = refs[4 : 4 + LEVEL_REFS]
    nat_q, nat_n, q_r, n_r, rhs, wsum, pack = refs[4 + LEVEL_REFS :]
    rows, ext, tiles = shape.rows, shape.ext_rows, shape.tiles
    level0, *levels = as_levels(level_refs)

    even, at_end = position("row")
    below, above = rows, ext - ROW_HALO
    met = pl.ds(aligned(jnp.where(even, below, above)), ROW_HALO)
    other = pl.ds(aligned(jnp.where(even, above, below)), ROW_HALO)
    for t in range(tiles + 1):
        lanes = slice(t * LANE, (t + 1) * LANE) if t < tiles else slice(0, LANE)
        own_q, own_n, from_even, from_odd = (
            (quality, counts, row_even, row_odd) if t < tiles else (edge_q, edge_n, corner_even, corner_odd)
        )
        for nat, own, start in ((nat_q, own_q, 0), (nat_n, own_n, ROW_HALO)):
            nat[t, 0:rows, :] = own[:, lanes]
            nat[t, met, :] = from_even[start : start + ROW_HALO, lanes]
            nat[t, other, :] = jnp.where(at_end, 0.0, from_odd[start : start + ROW_HALO, lanes])
            if ext > rows + 2 * ROW_HALO:
                gap = slice(rows + ROW_HALO, ext - ROW_HALO)
                nat[t, gap, :] = jnp.zeros_like(nat[t, gap, :])
    count = shape.chunk

    def relay(i, carry, put):
        rows_of = pl.ds(i, SUB, stride=shape.chunk)
        put(q_r, i, jnp.concatenate([nat_q[t, rows_of, :] for t in range(tiles + 1)], axis=1))
        put(n_r, i, jnp.concatenate([nat_n[t, rows_of, :] for t in range(tiles + 1)], axis=1))
        return carry

    run(count, relay, 0, UNROLL_TOP)
    close(q_r, count)
    close(n_r, count)

    def down_part(i):
        a = jnp.minimum(q_r[i], q_r[i + 1])
        sd = wrap_steps(n_r[i + 1] - n_r[i])
        return a, sd, -(a * sd)

    def step(i, carry, put):
        a_prev, gd_prev = carry
        a, sd, gd = down_part(i)
        q, n = q_r[i], n_r[i]
        b, bl = jnp.minimum(q, right_of(q, 1)), jnp.minimum(q, left_of(q, 1))
        sr, sl = wrap_steps(right_of(n, 1) - n), wrap_steps(n - left_of(n, 1))
        gr, gl = -(b * sr), -(bl * sl)
        w = relax_weight(a + a_prev + b + bl)
        put_level(put, level0, i, a, b, gd, gr, w, w * (gd - gd_prev + gr - gl), bl, gl)
        put(sd_r, i, sd)
        put(sr_r, i, sr)
        put(sl_r, i, sl)
        return a, gd

    a, _, gd = down_part(count - 1)
    run(count, step, (chunk_above(a), chunk_above(gd)), UNROLL_TOP)
    close(level0["est"], count)
    levels_down(level0, levels, dict(est=rhs, w=wsum), pack, out, shape)


def middle_kernel(*refs, shape):
    gathered, tables, (sd_r, sr_r, sl_r) = refs[0], refs[1:4], refs[4:7]
    old = as_levels(refs[7 : 7 + LEVEL_REFS])
    refs = refs[7 + LEVEL_REFS :]
    out, first = refs[:2]
    level0, *levels = as_levels(refs[2 : 2 + LEVEL_REFS])
    rhs, wsum, pack, corr, *results = refs[2 + LEVEL_REFS :]
    coarse_correction(gathered, tables, shape, corr)
    field = levels_up(old[1:], corr, results, shape)

    def emit(put, i, value):
        put(first, i, value)

    count = shape.chunk
    go_up(old[0], field, 0, shape, emit)
    close(first, count)
    a_old, b_old, bl_old = (old[0][k] for k in ("a", "b", "bl"))

    def reweighted(weight, error):
        weight = weight / jnp.maximum(jnp.abs(error), error_floor)
        return weight, weight * error

    def down_part(i):
        return reweighted(a_old[i], first[i + 1] - first[i] - sd_r[i])

    def step(i, carry, put):
        a_prev, gd_prev = carry
        a, gd = down_part(i)
        v = first[i]
        b, gr = reweighted(b_old[i], right_of(v, 1) - v - sr_r[i])
        bl, gl = reweighted(bl_old[i], v - left_of(v, 1) - sl_r[i])
        w = relax_weight(a + a_prev + b + bl)
        put_level(put, level0, i, a, b, gd, gr, w, w * (gd - gd_prev + gr - gl), bl, gl)
        return a, gd

    a, gd = down_part(count - 1)
    run(count, step, (chunk_above(a), chunk_above(gd)), UNROLL_TOP)
    close(level0["est"], count)
    levels_down(level0, levels, dict(est=rhs, w=wsum), pack, out, shape)


def end_kernel(*refs, shape):
    gathered, tables, first = refs[0], refs[1:4], refs[4]
    old = as_levels(refs[5 : 5 + LEVEL_REFS])
    out, nat, corr, *results = refs[5 + LEVEL_REFS :]
    coarse_correction(gathered, tables, shape, corr)
    field = levels_up(old[1:], corr, results, shape)

    def emit(put, i, value):
        value = value + first[i]
        for t in range(shape.tiles):
            place = (t, pl.ds(i, SUB, stride=shape.chunk), slice(None))
            put(nat, place, value[:, t * LANE : (t + 1) * LANE])

    go_up(old[0], field, 0, shape, emit)
    for t in range(shape.tiles):
        out[:, t * LANE : (t + 1) * LANE] = nat[t, 0 : shape.rows, :]


def dct_table(count):
    freq = np.arange(count)[:, None]
    place = np.arange(count)[None, :]
    table = np.cos(np.pi * (((2 * place + 1) * freq) % (4 * count)) / (2 * count)) * np.sqrt(2.0 / count)
    table[0] *= np.sqrt(0.5)
    return table.astype(np.float32)


def in_parts(x, count):
    x = np.asarray(x, np.float32)
    parts = []
    for _ in range(count):
        part = x.astype(jnp.bfloat16)
        x = x - part.astype(np.float32)
        parts.append(part)
    return np.concatenate(parts, axis=0)


def solve_tables(shape):
    gr, gc, per, crows, ccols = shape.grid_rows, shape.grid_cols, shape.per_chunk, shape.crows, shape.ccols
    fold, group, height = shape.fold, shape.group, shape.block_rows
    table_x, table_y = dct_table(gr), dct_table(gc)
    g, r, f, q = (
        x.ravel()
        for x in np.meshgrid(*map(np.arange, (group, shape.row_count, fold, height)), indexing="ij")
    )
    local = group * q + g
    inside = local < crows
    rows = table_x[:, np.where(inside, r * crows + local, 0)]
    forward = np.concatenate([np.where(inside & (f == n), rows, 0) for n in range(fold)], axis=0)
    f, c, j = (
        x.ravel() for x in np.meshgrid(*map(np.arange, (fold, shape.col_count // fold, ccols)), indexing="ij")
    )
    columns = table_y[:, (c * fold + f) * ccols + j].T
    slab, chunk = (x.ravel() for x in np.meshgrid(np.arange(per), np.arange(SUB), indexing="ij"))
    local = chunk * per + slab
    slots = SUB * per
    local = np.where(local < slots - ROW_HALO // CELL, local, local - slots)
    backward = [table_x.T[np.clip(r * crows + local, 0, gr - 1)] for r in range(shape.row_count)]
    width = -(-max(forward.shape[1], gr) // LANE) * LANE
    row_tables = [in_parts(forward, 3)] + [in_parts(x, 2) for x in backward]
    row_tables = np.concatenate([np.pad(x, ((0, 0), (0, width - x.shape[1]))) for x in row_tables], axis=0)
    transforms = np.concatenate([in_parts(columns, 3), in_parts(table_y, 2)], axis=0)
    lam_x = 2 - 2 * np.cos(np.pi * np.arange(gr) / gr)
    lam_y = 2 - 2 * np.cos(np.pi * np.arange(gc) / gc)
    inverse = 1 / (lam_x[:, None] + lam_y[None, :] + (screen_width / gc) ** 2)
    return [jnp.asarray(transforms), jnp.asarray(row_tables), jnp.asarray(inverse, jnp.float32)]


def f32(*dims):
    return jax.ShapeDtypeStruct(dims, jnp.float32)


def level_shapes(shape):
    return [
        f32(shape.slabs(d) + (key == "est"), SUB, shape.lanes)
        for d in range(GRIDS)
        for key in (LEVEL_KEYS if d else TOP_KEYS)
    ]


def vmem(*dims):
    return pltpu.VMEM(dims, jnp.float32)


def swap(even_strip, odd_strip, axis):
    rows, cols = lax.axis_size("row"), lax.axis_size("col")
    even_pairs, odd_pairs = [], []
    for r in range(rows):
        for c in range(cols):
            here = r * cols + c
            index, count, step = (r, rows, cols) if axis == "row" else (c, cols, 1)
            even_pairs.append((here, here + step * ((index ^ 1) - index)))
            if 0 < index < count - 1:
                odd_pairs.append((here, here + (step if index % 2 else -step)))
            else:
                odd_pairs.append((here, idle_pair(axis, r, c, rows, cols)))
    both = ("row", "col")
    return lax.ppermute(even_strip, both, even_pairs), lax.ppermute(odd_strip, both, odd_pairs)


def idle_pair(axis, r, c, rows, cols):
    if axis == "col":
        return (r ^ 1) * cols + c
    return (rows - 1 - r) * cols + c


def gather(blocks):
    blocks = lax.all_to_all(blocks, ("row", "col"), split_axis=0, concat_axis=0, tiled=True)
    return blocks.reshape(-1, SUB, LANE)


def body(swath, coherence, phase_counts, *, shape):
    params = pltpu.CompilerParams(vmem_limit_bytes=16 * 2**20)
    rows, cols = shape.rows, shape.cols
    block = f32(shape.row_count * shape.col_count, shape.block_rows, LANE)
    tables = solve_tables(shape)
    coarse_scratch = [vmem(shape.per_chunk, SUB, shape.lanes)] * 2 + [vmem(shape.per_chunk, SUB, LANE)]
    result_scratch = [vmem(shape.per_chunk + 1, SUB, shape.lanes)]
    result_scratch += [vmem(shape.slabs(d) + 1, SUB, shape.lanes) for d in range(1, GRIDS)]

    strip, edge, corner = f32(2 * ROW_HALO, cols), f32(rows, LANE), f32(2 * ROW_HALO, LANE)
    quality, counts, row_even, row_odd, col_even, col_odd = pl.pallas_call(
        strips_kernel,
        in_specs=[pl.BlockSpec(memory_space=pltpu.HBM)] * 3,
        out_shape=[f32(rows, cols), f32(rows, cols), strip, strip, edge, edge],
        scratch_shapes=[pltpu.VMEM((rows, cols), jnp.int32)] * 3 + [pltpu.SemaphoreType.DMA((3,))],
        compiler_params=params,
        name="strips",
    )(*(pltpu.with_memory_space_constraint(x, pltpu.HBM) for x in (swath, coherence, phase_counts)))
    row_even, row_odd = swap(row_even, row_odd, "row")
    col_even, col_odd = swap(col_even, col_odd, "col")
    edge_q, edge_n, corner_even, corner_odd = pl.pallas_call(
        corner_kernel,
        out_shape=[edge, edge, corner, corner],
        compiler_params=params,
        name="corners",
    )(col_even, col_odd)
    corner_even, corner_odd = swap(corner_even, corner_odd, "row")

    slabs = (shape.chunk, SUB, shape.lanes)
    more = (shape.chunk + 1, SUB, shape.lanes)
    nat = vmem(shape.tiles, shape.ext_rows, LANE)
    wide = vmem(shape.tiles + 1, shape.ext_rows, LANE)
    block_out, sd, sr, sl, *old = pl.pallas_call(
        functools.partial(start_kernel, shape=shape),
        out_shape=[block] + [f32(*slabs)] * 3 + level_shapes(shape),
        scratch_shapes=[wide, wide, vmem(*more), vmem(*more)] + coarse_scratch,
        compiler_params=params,
        name="start",
    )(quality, counts, row_even, row_odd, edge_q, edge_n, corner_even, corner_odd, tables[2])
    gathered = gather(block_out)
    block_out, first, *old = pl.pallas_call(
        functools.partial(middle_kernel, shape=shape),
        out_shape=[block, f32(*more)] + level_shapes(shape),
        scratch_shapes=coarse_scratch + result_scratch,
        compiler_params=params,
        name="middle",
    )(gathered, *tables, sd, sr, sl, *old)
    gathered = gather(block_out)
    return pl.pallas_call(
        functools.partial(end_kernel, shape=shape),
        out_shape=f32(rows, cols),
        scratch_shapes=[nat] + result_scratch,
        compiler_params=params,
        name="finish",
    )(gathered, *tables, first, *old)


def solution(mesh):
    def run(swath, coherence, phase_counts):
        rows, cols = swath.shape
        row_count, col_count = mesh.shape["row"], mesh.shape["col"]
        shape = Shape(rows // row_count, cols // col_count, row_count, col_count)
        return jax.shard_map(
            functools.partial(body, shape=shape),
            mesh=mesh,
            in_specs=(P("row", "col"), P("row", "col"), P("row", "col")),
            out_specs=P("row", "col"),
            check_vma=False,
        )(swath, coherence, phase_counts)

    return run
```

time: 56.8 us -> 49.3 us (0.87)
  Pallas kernels: 20.5 us -> 15.3 us
  blocking collectives: 23.2 us -> 21.7 us
  local copies, waits for them, and re-layouts: 0.78 us -> 0.02 us
    pallas_call x1, Pallas kernels: 8.31 us -> 5.75 us  [body(): pl.pallas_call(functools.partial(middle_kernel, shape=shape), out_shape=[...]
    pallas_call x1, Pallas kernels: 6.86 us -> 4.57 us  [body(): pl.pallas_call(functools.partial(start_kernel, shape=shape), out_shape=[b...]
    all_to_all x2, blocking collectives: 23.2 us -> 21.7 us  [gather(): lax.all_to_all(blocks, ('row', 'col'), split_axis=0, concat_axis=0, tiled...]
    unnamed x8 -> x6, local copies, waits for them, and re-layouts: 0.78 us -> 0.02 us
where the time goes in v4:
time: 49.3 us; the launch traced here: 49.1 us
  blocking collectives  21.7 us (44%)
  Pallas kernels  15.3 us (31%)
  waiting for transfers between devices  6.73 us (14%)
  starting transfers between devices  5.34 us (11%)
    all_to_all x2, blocking collectives, gather(): lax.all_to_all(blocks, ('row', 'col'), split_axis=0, concat_axis=0, tiled...  21.7 us
    pallas_call x1, Pallas kernels, body(): pl.pallas_call(functools.partial(middle_kernel, shape=shape), out_shape=[...  5.75 us
    pallas_call x1, Pallas kernels, body(): pl.pallas_call(functools.partial(start_kernel, shape=shape), out_shape=[b...  4.57 us
    ppermute x3, waiting for transfers between devices, swap(): lax.ppermute(even_strip, both, even_pairs)  4.36 us
    pallas_call x1, Pallas kernels, body(): pl.pallas_call(functools.partial(end_kernel, shape=shape), out_shape=f32(...  3.52 us
    ppermute x3, starting transfers between devices, swap(): lax.ppermute(odd_strip, both, odd_pairs)  3.2 us
    ppermute x3, waiting for transfers between devices, swap(): lax.ppermute(odd_strip, both, odd_pairs)  2.37 us
    ppermute x3, starting transfers between devices, swap(): lax.ppermute(even_strip, both, even_pairs)  2.15 us
  transfers between devices with their start and end apart: 6, of which 3 were waited for; matrix products, arithmetic and copies ran while one was open for 0% of the time, Pallas kernels for 0%

profile of v4, /device:TPU:0, one launch (start us, length us, event | category | flops | bytes accessed | tf_op | source)
XLA Modules:
  0.0 49.1 jit_solution(11496406661220374645)
XLA Ops:
  0.0 1.4 %strips.1 = (f32[160,512]{1,0:T(8,128)S(1)}, f32[160,512]{1,0:T(8,128)S(1)}, f32[96,512]{1,0:T(8,128)S(1)}, f32[96,512]{1,0:T(8,128)S(1)}, f32[160,128]{1,0:T(8,128)S(1)}, /*index=5*/f32[160,128]{1,0:T(8,128)S(1)}) custom-call(s32[160,512]{1,0:T(8,128)} %swath.1, s32[160,512]{1,0:T(8,128)} %coherence.1, s32[160,512]{1,0:T(8,128)} %counts.1), custom_call_target="tpu_custom_call" | custom-call | tf_op jit(solution)/shard_map/strips/pallas_call | solution.py:626
  1.4 0.6 %collective-permute-start = (f32[96,512]{1,0:T(8,128)S(1)}, f32[96,512]{1,0:T(8,128)S(1)}, u32[]{:S(2)}, u32[]{:S(2)}) collective-permute-start(f32[96,512]{1,0:T(8,128)S(1)} %get-tuple-element.75), channel_id=1, source_target_pairs={{0,8},{1,9},{2,10},{3,11},{4,12},{5,13},{6,14},{7,15},{8,0},{9,1},... | collective-permute-start | bytes 589832 | tf_op jit(solution)/shard_map/ppermute | solution.py:602
  1.9 2.6 %collective-permute-start.1 = (f32[96,512]{1,0:T(8,128)S(1)}, f32[96,512]{1,0:T(8,128)S(1)}, u32[]{:S(2)}, u32[]{:S(2)}) collective-permute-start(f32[96,512]{1,0:T(8,128)S(1)} %get-tuple-element.76), channel_id=1, source_target_pairs={{0,24},{1,25},{2,26},{3,27},{4,28},{5,29},{6,30},{7,31},{8,16},{9,... | collective-permute-start | bytes 589832 | tf_op jit(solution)/shard_map/ppermute | solution.py:602
  4.5 1.5 %collective-permute-start.2 = (f32[160,128]{1,0:T(8,128)S(1)}, f32[160,128]{1,0:T(8,128)S(1)}, u32[]{:S(2)}, u32[]{:S(2)}) collective-permute-start(f32[160,128]{1,0:T(8,128)S(1)} %get-tuple-element.77), channel_id=1, source_target_pairs={{0,1},{1,0},{2,3},{3,2},{4,5},{5,4},{6,7},{7,6},{8,9},{9,8},{10,11... | collective-permute-start | bytes 245768 | tf_op jit(solution)/shard_map/ppermute | solution.py:602
  6.0 0.0 copy-start.2
  6.0 0.0 collective-permute-start.3
  6.1 3.7 %collective-permute-done.2.col_even = f32[160,128]{1,0:T(8,128)S(1)} collective-permute-done((f32[160,128]{1,0:T(8,128)S(1)}, f32[160,128]{1,0:T(8,128)S(1)}, u32[]{:S(2)}, u32[]{:S(2)}) %collective-permute-start.2) | collective-permute-done | bytes 81952 | tf_op jit(solution)/shard_map/ppermute | solution.py:602
  9.8 0.0 collective-permute-done.3.col_odd
  9.8 0.1 corners.1
  9.9 0.1 collective-permute-start.4
  10.0 0.6 %collective-permute-start.5 = (f32[96,128]{1,0:T(8,128)S(1)}, f32[96,128]{1,0:T(8,128)S(1)}, u32[]{:S(2)}, u32[]{:S(2)}) collective-permute-start(f32[96,128]{1,0:T(8,128)S(1)} %get-tuple-element.82), channel_id=1, source_target_pairs={{0,24},{1,25},{2,26},{3,27},{4,28},{5,29},{6,30},{7,31},{8,16},{9,... | collective-permute-start | bytes 147464 | tf_op jit(solution)/shard_map/ppermute | solution.py:602
  10.6 0.6 %collective-permute-done.4.refs_6_ = f32[96,128]{1,0:T(8,128)S(1)} collective-permute-done((f32[96,128]{1,0:T(8,128)S(1)}, f32[96,128]{1,0:T(8,128)S(1)}, u32[]{:S(2)}, u32[]{:S(2)}) %collective-permute-start.4) | collective-permute-done | bytes 49184 | tf_op jit(solution)/shard_map/ppermute | solution.py:602
  11.2 2.4 %collective-permute-done.5.refs_7_ = f32[96,128]{1,0:T(8,128)S(1)} collective-permute-done((f32[96,128]{1,0:T(8,128)S(1)}, f32[96,128]{1,0:T(8,128)S(1)}, u32[]{:S(2)}, u32[]{:S(2)}) %collective-permute-start.5) | collective-permute-done | bytes 49184 | tf_op jit(solution)/shard_map/ppermute | solution.py:602
  13.6 0.0 collective-permute-done.refs_2_
  13.6 0.0 collective-permute-done.1.refs_3_
  13.6 0.0 copy-done.2
  13.6 0.0 copy-start
  13.6 4.6 %start.1 = (f32[32,4,128]{2,1,0:T(4,128)S(1)}, f32[32,8,640]{2,1,0:T(8,128)S(1)}, f32[32,8,640]{2,1,0:T(8,128)S(1)}, f32[32,8,640]{2,1,0:T(8,128)S(1)}, f32[32,8...) custom-call(f32[160,512]{1,0:T(8,128)S(1)} %get-tuple-element.73.ref, ...), custom_call_target="tpu_custom_call" | custom-call | tf_op jit(solution)/shard_map/start/pallas_call | solution.py:648
  18.2 0.0 copy-start.1
  18.2 12.7 %all_to_all.10 = f32[32,4,128]{2,1,0:T(4,128)S(1)} all-to-all(f32[32,4,128]{2,1,0:T(4,128)S(1)} %get-tuple-element.83), channel_id=1, replica_groups=mesh['row'=4,'col'=8] {'row','col'}, dimensions={0} | all-to-all | bytes 131072 | tf_op jit(solution)/shard_map/all_to_all | solution.py:612
  30.9 0.0 copy-done
  30.9 0.0 copy-done.1
  30.9 5.7 %middle.1 = (f32[32,4,128]{2,1,0:T(4,128)S(1)}, f32[33,8,640]{2,1,0:T(8,128)S(1)}, f32[32,8,640]{2,1,0:T(8,128)S(1)}, f32[32,8,640]{2,1,0:T(8,128)S(1)}, f32[32,...) custom-call(f32[16,8,128]{2,1,0:T(8,128)S(1)} %bitcast.2, ...), custom_call_target="tpu_custom_call" | custom-call | tf_op jit(solution)/shard_map/middle/pallas_call | solution.py:656
  36.6 9.0 %all_to_all.11 = f32[32,4,128]{2,1,0:T(4,128)S(1)} all-to-all(f32[32,4,128]{2,1,0:T(4,128)S(1)} %get-tuple-element.113), channel_id=1, replica_groups=mesh['row'=4,'col'=8] {'row','col'}, dimensions={0} | all-to-all | bytes 131072 | tf_op jit(solution)/shard_map/all_to_all | solution.py:612
  45.6 3.5 %finish.1 = f32[160,512]{1,0:T(8,128)} custom-call(f32[16,8,128]{2,1,0:T(8,128)S(1)} %bitcast.3, bf16[1280,256]{1,0:T(8,128)(2,1)S(1)} %copy-done, bf16[368,128]{1,0:T(8,128)(2,1)S(1)} %copy-done.1, f32[40,256]{1,0:T(8,128)S(1)} %copy-done.2, f32[33,8,640]{2,1,0:T(8,128)S(1)} %get-tuple-element.114.refs_4_, f32[32,8,640]{2,1,0:T(8,128)S(1)} %get-tuple-element.115.refs_5_, ...), custom_call_target="tpu_custom_call" | custom-call | tf_op jit(solution)/shard_map/finish/pallas_call | solution.py:664
Async XLA Ops:
  1.4 12.2 %collective-permute-start = (f32[96,512]{1,0:T(8,128)S(1)}, f32[96,512]{1,0:T(8,128)S(1)}, u32[]{:S(2)}, u32[]{:S(2)}) collective-permute-start(f32[96,512]{1,0:T(8,128)S(1)} %get-tuple-element.75), channel_id=1, source_target_pairs={{0,8},{1,9},{2,10},{3,11},{4,12},{5,13},{6,14},{7,15},{8,0},{9,1},... | collective-permute-start | bytes 589832 | tf_op jit(solution)/shard_map/ppermute | solution.py:602
  1.9 11.6 %collective-permute-start.1 = (f32[96,512]{1,0:T(8,128)S(1)}, f32[96,512]{1,0:T(8,128)S(1)}, u32[]{:S(2)}, u32[]{:S(2)}) collective-permute-start(f32[96,512]{1,0:T(8,128)S(1)} %get-tuple-element.76), channel_id=1, source_target_pairs={{0,24},{1,25},{2,26},{3,27},{4,28},{5,29},{6,30},{7,31},{8,16},{9,... | collective-permute-start | bytes 589832 | tf_op jit(solution)/shard_map/ppermute | solution.py:602
  4.5 5.3 %collective-permute-start.2 = (f32[160,128]{1,0:T(8,128)S(1)}, f32[160,128]{1,0:T(8,128)S(1)}, u32[]{:S(2)}, u32[]{:S(2)}) collective-permute-start(f32[160,128]{1,0:T(8,128)S(1)} %get-tuple-element.77), channel_id=1, source_target_pairs={{0,1},{1,0},{2,3},{3,2},{4,5},{5,4},{6,7},{7,6},{8,9},{9,8},{10,11... | collective-permute-start | bytes 245768 | tf_op jit(solution)/shard_map/ppermute | solution.py:602
  6.0 7.5 %copy-start.2 = (f32[40,256]{1,0:T(8,128)S(1)}, f32[40,256]{1,0:T(8,128)}, u32[]{:S(2)}) copy-start(f32[40,256]{1,0:T(8,128)} %constant.8.clone.refs_8_.refs_3_) | copy-start | bytes 122884
  6.0 3.7 %collective-permute-start.3 = (f32[160,128]{1,0:T(8,128)S(1)}, f32[160,128]{1,0:T(8,128)S(1)}, u32[]{:S(2)}, u32[]{:S(2)}) collective-permute-start(f32[160,128]{1,0:T(8,128)S(1)} %get-tuple-element.78), channel_id=1, source_target_pairs={{0,8},{1,2},{2,1},{3,4},{4,3},{5,6},{6,5},{7,15},{8,0},{9,10},{10,... | collective-permute-start | bytes 245768 | tf_op jit(solution)/shard_map/ppermute | solution.py:602
  9.9 1.3 %collective-permute-start.4 = (f32[96,128]{1,0:T(8,128)S(1)}, f32[96,128]{1,0:T(8,128)S(1)}, u32[]{:S(2)}, u32[]{:S(2)}) collective-permute-start(f32[96,128]{1,0:T(8,128)S(1)} %get-tuple-element.81), channel_id=1, source_target_pairs={{0,8},{1,9},{2,10},{3,11},{4,12},{5,13},{6,14},{7,15},{8,0},{9,1},... | collective-permute-start | bytes 147464 | tf_op jit(solution)/shard_map/ppermute | solution.py:602
  10.0 3.6 %collective-permute-start.5 = (f32[96,128]{1,0:T(8,128)S(1)}, f32[96,128]{1,0:T(8,128)S(1)}, u32[]{:S(2)}, u32[]{:S(2)}) collective-permute-start(f32[96,128]{1,0:T(8,128)S(1)} %get-tuple-element.82), channel_id=1, source_target_pairs={{0,24},{1,25},{2,26},{3,27},{4,28},{5,29},{6,30},{7,31},{8,16},{9,... | collective-permute-start | bytes 147464 | tf_op jit(solution)/shard_map/ppermute | solution.py:602
  13.6 17.3 %copy-start = (bf16[1280,256]{1,0:T(8,128)(2,1)S(1)}, bf16[1280,256]{1,0:T(8,128)(2,1)}, u32[]{:S(2)}) copy-start(bf16[1280,256]{1,0:T(8,128)(2,1)} %constant.6.clone.refs_1_) | copy-start | bytes 1966084
  18.2 12.7 %copy-start.1 = (bf16[368,128]{1,0:T(8,128)(2,1)S(1)}, bf16[368,128]{1,0:T(8,128)(2,1)}, u32[]{:S(2)}) copy-start(bf16[368,128]{1,0:T(8,128)(2,1)} %constant.7.clone.refs_2_) | copy-start | bytes 282628
